TPU v7x, 256 devices: a whole 4x4x8 slice. The times are simulated.
256 devices in a mesh: top: 4 (over x_lo, core), mid: 2 (over x_hi), leaf: 32 (over y, z).
Axes of the slice: x: 4 (x_hi: 2, x_lo: 2; x = x_hi * 2 + x_lo), y: 4, z: 8, core: 2. Of those that a mesh axis runs over, the one named last changes fastest.
Arguments:
- rhs: bfloat16 [393216, 256], P(('top', 'mid', 'leaf')), may hold values from -6 to 6
- guess: bfloat16 [393216, 256], P(('top', 'mid', 'leaf')), may hold values from -3 to 3
- diag_blocks: bfloat16 [256, 1536, 1536], P(('top', 'mid', 'leaf')), as said below
- precond: bfloat16 [256, 1536, 1536], P(('top', 'mid', 'leaf'))
- bases: bfloat16 [256, 1536, 128], P(('top', 'mid', 'leaf')), may hold values from -0.3125 to 0.3125
- leaf_to_middle_transfer: bfloat16 [256, 128, 128], P(('top', 'mid', 'leaf')), may hold values from -0.25 to 0.25
- mid_transfer: bfloat16 [8, 128, 128], replicated, may hold values from -0.375 to 0.375
- leaf_coupling: bfloat16 [256, 4, 128, 128], P(('top', 'mid', 'leaf')), may hold values from -0.25 to 0.25
- cluster_coupling: bfloat16 [8, 3, 128, 128], P(('top', 'mid')), may hold values from -0.3125 to 0.3125
- group_coupling: bfloat16 [4, 2, 128, 128], P('top'), may hold values from -0.375 to 0.375
- leaf_lists: int32 [256, 4], P(('top', 'mid', 'leaf')), may hold values from 0 to 31, as said below
- owner: int32 [8, 32], P(('top', 'mid')), may hold values from 0 to 31, as said below
- cluster_lists: int32 [8, 3], P(('top', 'mid')), may hold values from 0 to 7, as said below
- group_lists: int32 [4, 2], P('top'), may hold values from 0 to 3, as said below
Outputs:
- solution: bfloat16 [393216, 256], P(('top', 'mid', 'leaf'))
Inputs may be any that keep to these rules, and one draw needn't show every extreme that they name: `leaf_lists`: each row holds 4 distinct sibling cluster ids. `owner`: each row is a permutation of the slots of the cluster. `cluster_lists`: each row holds 3 distinct cluster ids. `group_lists`: each row holds 2 distinct group ids. `diag_blocks`: each block is a diagonal with entries from 1 to 3 plus small dense noise.
All inputs are finite; a program needn't handle non-finite values.
Results may differ from a plain program's by a relative error of at most 0.028.
Values may be sent and summed in bfloat16 or wider, within the bound.
A program may use at most 64 MiB of HBM per device.

v0:
```python
import jax
import jax.numpy as jnp
from jax import lax
from jax.sharding import PartitionSpec as P

damping = 0.7


def sent_together(arrays, axis, dim, along):
    ends, at = ([], 0)
    for a in arrays[:-1]:
        at += a.shape[along]
        ends.append(at)
    both = jnp.concatenate(arrays, axis=along)
    return tuple(jnp.split(lax.all_gather(both, axis, axis=dim, tiled=True), ends, axis=along))


def copy_for_each(value, axis):
    copies = jnp.broadcast_to(value, (lax.axis_size(axis), *value.shape))
    return lax.all_to_all(copies, axis, split_axis=0, concat_axis=0, tiled=True)


def laid_out(blocks, dim):
    blocks = jnp.moveaxis(blocks, 0, dim)
    shape = blocks.shape
    return blocks.reshape(*shape[:dim], shape[dim] * shape[dim + 1], *shape[dim + 2 :])


def gather_directly(value, axis, dim):
    blocks = copy_for_each(value, axis)
    return laid_out(blocks, dim)


def far_field(
    vector,
    bases,
    leaf_to_middle_transfer,
    mid_transfer,
    leaf_coupling,
    cluster_coupling,
    group_coupling,
    slots,
    cluster_lists,
    group_lists,
):
    single_precision = jnp.float32
    brain_float_sixteen = jnp.bfloat16
    rank = bases.shape[2]
    columns = vector.shape[1]
    leaf_coefficient = jnp.einsum(
        "na,nr->ar", bases[0], vector, preferred_element_type=single_precision
    ).astype(brain_float_sixteen)
    upward_contribution = jnp.einsum(
        "ba,br->ar",
        leaf_to_middle_transfer[0],
        leaf_coefficient,
        preferred_element_type=single_precision,
    ).astype(brain_float_sixteen)
    sibling_coefs, sibling_terms = sent_together(
        (leaf_coefficient, upward_contribution), "leaf", 0, 1
    )
    sibling_coefs = sibling_coefs.reshape(-1, rank, columns)
    cluster_coef = jnp.sum(
        sibling_terms.astype(single_precision).reshape(-1, rank, columns), axis=0
    )
    cluster_half = cluster_coef.astype(brain_float_sixteen)
    cluster_index = lax.axis_index(("top", "mid"))
    own_transfer = lax.dynamic_index_in_dim(mid_transfer, cluster_index, 0, keepdims=False)
    all_clusters = gather_directly(cluster_half, ("top", "mid"), 0).reshape(-1, rank, columns)
    group_terms = jnp.einsum(
        "cba,cbr->car", mid_transfer, all_clusters, preferred_element_type=single_precision
    )
    group_coefs = jnp.sum(
        group_terms.reshape(-1, lax.axis_size("mid"), rank, columns), axis=1
    ).astype(brain_float_sixteen)
    group_far = jnp.einsum(
        "kab,kbr->ar",
        group_coupling[0],
        jnp.take(group_coefs, group_lists[0], axis=0),
        preferred_element_type=single_precision,
    )
    cluster_far = jnp.einsum(
        "kab,kbr->ar",
        cluster_coupling[0],
        jnp.take(all_clusters, cluster_lists[0], axis=0),
        preferred_element_type=single_precision,
    )
    picked = jnp.take(sibling_coefs, slots, axis=0)
    leaf_distant_field = jnp.einsum(
        "kab,kbr->ar", leaf_coupling[0], picked, preferred_element_type=single_precision
    )
    cluster_total = (
        cluster_far
        + jnp.dot(
            own_transfer,
            group_far.astype(brain_float_sixteen),
            preferred_element_type=single_precision,
        )
    ).astype(brain_float_sixteen)
    leaf_grand_total = (
        leaf_distant_field
        + jnp.dot(
            leaf_to_middle_transfer[0], cluster_total, preferred_element_type=single_precision
        )
    ).astype(brain_float_sixteen)
    return jnp.dot(bases[0], leaf_grand_total, preferred_element_type=single_precision)


def body(
    rhs,
    guess,
    diag_blocks,
    precond,
    bases,
    leaf_to_middle_transfer,
    mid_transfer,
    leaf_coupling,
    cluster_coupling,
    group_coupling,
    leaf_lists,
    owner,
    cluster_lists,
    group_lists,
):
    slots = jnp.take(owner[0], leaf_lists[0], axis=0)

    def apply_matrix(vector):
        near_part = jnp.dot(diag_blocks[0], vector, preferred_element_type=jnp.float32)
        return near_part + far_field(
            vector,
            bases,
            leaf_to_middle_transfer,
            mid_transfer,
            leaf_coupling,
            cluster_coupling,
            group_coupling,
            slots,
            cluster_lists,
            group_lists,
        )

    def smooth(residual):
        return jnp.dot(
            precond[0], residual.astype(jnp.bfloat16), preferred_element_type=jnp.float32
        )

    target = rhs.astype(jnp.float32)
    residual = target - apply_matrix(guess)
    first = guess.astype(jnp.float32) + damping * smooth(residual)
    residual = target - apply_matrix(first.astype(jnp.bfloat16))
    second = first + damping * smooth(residual)
    return second.astype(jnp.bfloat16)


def solution(mesh):
    in_specs = (
        P(("top", "mid", "leaf"), None),
        P(("top", "mid", "leaf"), None),
        P(("top", "mid", "leaf"), None, None),
        P(("top", "mid", "leaf"), None, None),
        P(("top", "mid", "leaf"), None, None),
        P(("top", "mid", "leaf"), None, None),
        P(),
        P(("top", "mid", "leaf"), None, None, None),
        P(("top", "mid"), None, None, None),
        P("top", None, None, None),
        P(("top", "mid", "leaf"), None),
        P(("top", "mid"), None),
        P(("top", "mid"), None),
        P("top", None),
    )
    out_specs = P(("top", "mid", "leaf"), None)
    return jax.shard_map(body, mesh=mesh, in_specs=in_specs, out_specs=out_specs, check_vma=False)
```

profile of v0, /device:TPU:32, one launch (start us, length us, event | category | flops | bytes accessed | tf_op | source)
XLA Modules:
  0.0 251.3 jit_solution(7287898906119648909)
XLA Ops:
  6.6 0.9 copy-done
  7.5 1.5 convolution_convert_fusion.1
  9.0 1.0 fusion.41
  10.0 0.7 pad_maximum_fusion
  10.7 1.2 copy.33
  11.9 0.6 gather_fusion
  12.6 0.5 compare_and_fusion.1
  13.2 0.6 compare_and_fusion.2
  13.7 4.9 %fusion.6 = f32[1536,256]{1,0:T(8,128)} fusion(bf16[1536,256]{1,0:T(8,128)(2,1)S(1)} %copy-done.3, bf16[1,1536,1536]{2,1,0:T(8,128)(2,1)} %param.22), kind=kOutput, calls=%fused_computation.13 | convolution fusion | flops 1207959552 | bytes 7077888 | tf_op jit(solution)/shard_map/dot_general | solution.py:128
  18.6 76.3 %all-gather.3.cloned.1.call-done = bf16[4096,512]{1,0:T(8,128)(2,1)} async-done(((bf16[128,512]{1,0:T(8,128)(2,1)}), bf16[4096,512]{1,0:T(8,128)(2,1)}) %all-gather.3.cloned.1.call-update) | async-done | bytes 4194320 | tf_op jit(solution)/shard_map/all_gather | solution.py:15
  94.9 3.8 %fusion.102 = (bf16[4096,256]{1,0:T(8,128)(2,1)S(1)}, bf16[4096,256]{1,0:T(8,128)(2,1)}) fusion(bf16[4096,512]{1,0:T(8,128)(2,1)} %all-gather.3.cloned.1.call-done), kind=kLoop, calls=%fused_computation.118 | loop fusion | bytes 8388608 | tf_op jit(solution)/shard_map/split | solution.py:15
  98.7 0.3 reduce
  99.0 0.1 copy.36
  99.1 0.9 broadcast_in_dim.35
  100.0 4.3 %all-to-all-start = ((bf16[8,128,256]{1,2,0:T(8,128)(2,1)}), bf16[8,128,256]{1,2,0:T(8,128)(2,1)S(1)}, u32[]{:S(2)}, u32[]{:S(2)}) async-start(bf16[8,128,256]{1,2,0:T(8,128)(2,1)} %broadcast_in_dim.35), calls=%async_computation | async-start | bytes 1048576 | tf_op jit(solution)/shard_map/all_to_all | solution.py:20
  104.4 0.8 compare_and_fusion
  105.2 2.9 %gather_fusion.1 = bf16[4,128,256]{2,1,0:T(8,128)(2,1)} fusion(bf16[32,128,256]{2,1,0:T(8,128)(2,1)} %bitcast.169, s32[1024]{0:T(1024)S(1)} %pad_clamp_fusion.2), kind=kCustom, calls=%fused_computation.clone | custom fusion | bytes 524304 | tf_op jit(solution)/shard_map/jit(_take)/gather | solution.py:88
  108.0 2.0 convolution_bitcast_fusion.2
  110.0 3.9 %all-to-all-done = bf16[8,128,256]{1,2,0:T(8,128)(2,1)S(1)} async-done(((bf16[8,128,256]{1,2,0:T(8,128)(2,1)}), bf16[8,128,256]{1,2,0:T(8,128)(2,1)S(1)}, u32[]{:S(2)}, u32[]{:S(2)}) %all-to-all-start) | async-done | bytes 524320 | tf_op jit(solution)/shard_map/all_to_all | solution.py:20
  113.9 1.0 bitcast_reduce_fusion.2
  114.9 2.2 gather_fusion.3
  117.1 1.2 gather_fusion.2
  118.3 1.3 convolution_bitcast_fusion.6
  119.6 1.3 fusion.37
  120.9 2.4 fusion.33
  123.2 4.2 %fusion.24 = f32[1536,256]{0,1:T(8,128)S(1)} fusion(bf16[1536,256]{1,0:T(8,128)(2,1)} %fusion.33, bf16[1,1536,1536]{2,1,0:T(8,128)(2,1)} %param.23, bf16[1536,256]{0,1:T(8,128)(2,1)} %copy.33), kind=kOutput, calls=%fused_computation.25 | convolution fusion | flops 1209139200 | bytes 7864320 | tf_op jit(solution)/shard_map/dot_general | solution.py:143
  127.5 1.2 copy-done.6
  128.7 0.4 convolution_convert_fusion
  129.0 0.1 fusion.42
  129.2 0.7 pad_maximum_fusion.1
  129.9 78.9 %all-gather.5.cloned.1.call-done = bf16[4096,512]{0,1:T(8,128)(2,1)} async-done(((bf16[128,512]{0,1:T(8,128)(2,1)}), bf16[4096,512]{0,1:T(8,128)(2,1)}) %all-gather.5.cloned.1.call-update) | async-done | bytes 4194320 | tf_op jit(solution)/shard_map/all_gather | solution.py:15
  208.8 2.6 %slice_bitcast_fusion = (bf16[32,8,32,128]{3,1,2,0:T(8,128)(2,1)S(1)}, bf16[4096,256]{0,1:T(8,128)(2,1)S(1)}) fusion(bf16[4096,512]{0,1:T(8,128)(2,1)} %all-gather.5.cloned.1.call-done), kind=kLoop, calls=%fused_computation.31 | loop fusion | bytes 8388608
  211.4 0.5 copy.54
  211.9 1.0 bitcast_reduce_fusion
  212.9 0.9 broadcast_in_dim.36
  213.8 4.3 %all-to-all-start.1 = ((bf16[8,128,256]{1,2,0:T(8,128)(2,1)}), bf16[8,128,256]{1,2,0:T(8,128)(2,1)}, u32[]{:S(2)}, u32[]{:S(2)}) async-start(bf16[8,128,256]{1,2,0:T(8,128)(2,1)} %broadcast_in_dim.36), calls=%async_computation.1 | async-start | bytes 1048576 | tf_op jit(solution)/shard_map/all_to_all | solution.py:20
  218.1 5.4 %fusion.4 = f32[256,1536]{0,1:T(8,128)} fusion(bf16[1,1536,1536]{2,1,0:T(8,128)(2,1)} %param.22, f32[1536,256]{0,1:T(8,128)} %copy-done.6), kind=kOutput, calls=%fused_computation.11 | convolution fusion | flops 1208352768 | bytes 7864320 | tf_op jit(solution)/shard_map/dot_general | solution.py:128
  223.5 2.5 copy.53
  226.0 2.3 gather_fusion.4
  228.3 1.9 convolution_bitcast_fusion.1
  230.2 1.3 bitcast_reduce_fusion.1
  231.5 0.6 gather_fusion.6
  232.1 1.6 gather_fusion.5
  233.8 1.8 convolution_bitcast_fusion.4
  235.6 1.9 fusion.39
  237.5 1.5 fusion.34
  239.0 4.3 %fusion.30 = bf16[1536,256]{0,1:T(8,128)(2,1)S(1)} fusion(f32[1536,256]{0,1:T(8,128)} %copy-done.6, bf16[1536,256]{1,0:T(8,128)(2,1)S(1)} %fusion.34, bf16[1,1536,1536]{2,1,0:T(8,128)(2,1)} %param.23), kind=kOutput, calls=%fused_computation.27 | convolution fusion | flops 1209139200 | bytes 7864320 | tf_op jit(solution)/shard_map/dot_general | solution.py:143
  243.3 1.2 copy.44
  (38 shorter events, 0.2 us)
Async XLA Ops:
  6.5 1.0 copy-start
  6.5 4.1 %copy-start.3 = (bf16[1536,256]{1,0:T(8,128)(2,1)S(1)}, bf16[1536,256]{1,0:T(8,128)(2,1)}, u32[]{:S(2)}) copy-start(bf16[1536,256]{1,0:T(8,128)(2,1)} %param.21) | copy-start | bytes 2359300
  6.5 5.4 %copy-start.10 = (s32[1,4]{1,0:T(1,128)S(1)}, s32[1,4]{1,0:T(1,128)}, u32[]{:S(2)}) copy-start(s32[1,4]{1,0:T(1,128)} %param.30) | copy-start | bytes 52
  6.5 5.4 %copy-start.1 = (s32[1,32]{1,0:T(1,128)S(1)}, s32[1,32]{1,0:T(1,128)}, u32[]{:S(2)}) copy-start(s32[1,32]{1,0:T(1,128)} %param.31) | copy-start | bytes 388
  6.5 6.0 %copy-start.12 = (s32[1,2]{1,0:T(1,128)S(1)}, s32[1,2]{1,0:T(1,128)}, u32[]{:S(2)}) copy-start(s32[1,2]{1,0:T(1,128)} %param.33) | copy-start | bytes 28
  6.6 6.0 %copy-start.11 = (s32[1,3]{1,0:T(1,128)S(1)}, s32[1,3]{1,0:T(1,128)}, u32[]{:S(2)}) copy-start(s32[1,3]{1,0:T(1,128)} %param.32) | copy-start | bytes 40
  6.6 88.3 %all-gather.3.cloned.1.call-start = ((), (), s32[]{:S(2)}) async-start(), calls=%async_computation.2 | async-start | bytes 4325376 | tf_op jit(solution)/shard_map/all_gather | solution.py:15
  98.7 15.2 %copy-start.7 = (bf16[8,128,128]{2,1,0:T(8,128)(2,1)S(1)}, bf16[8,128,128]{2,1,0:T(8,128)(2,1)}, u32[]{:S(2)}) copy-start(bf16[8,128,128]{2,1,0:T(8,128)(2,1)} %param.26) | copy-start | bytes 786436
  100.0 13.9 %all-to-all-start = ((bf16[8,128,256]{1,2,0:T(8,128)(2,1)}), bf16[8,128,256]{1,2,0:T(8,128)(2,1)S(1)}, u32[]{:S(2)}, u32[]{:S(2)}) async-start(bf16[8,128,256]{1,2,0:T(8,128)(2,1)} %broadcast_in_dim.35), calls=%async_computation | async-start | bytes 1048576 | tf_op jit(solution)/shard_map/all_to_all | solution.py:20
  104.3 16.6 %copy-start.2 = (bf16[1536,256]{1,0:T(8,128)(2,1)S(1)}, bf16[1536,256]{1,0:T(8,128)(2,1)}, u32[]{:S(2)}) copy-start(bf16[1536,256]{1,0:T(8,128)(2,1)} %param.20) | copy-start | bytes 2359300
  104.3 16.6 %copy-start.4 = (f32[1536,256]{1,0:T(8,128)S(1)}, f32[1536,256]{1,0:T(8,128)}, u32[]{:S(2)}) copy-start(f32[1536,256]{1,0:T(8,128)} %fusion.6) | copy-start | bytes 4718596
  104.3 104.5 %all-gather.5.cloned.1.call-start = ((), (), s32[]{:S(2)}) async-start(), calls=%async_computation.3 | async-start | bytes 4325376 | tf_op jit(solution)/shard_map/all_gather | solution.py:15
  123.2 5.8 %copy-start.8 = (bf16[1,128,128]{2,1,0:T(8,128)(2,1)S(1)}, bf16[1,128,128]{2,1,0:T(8,128)(2,1)}, u32[]{:S(2)}) copy-start(bf16[1,128,128]{2,1,0:T(8,128)(2,1)} %param.25) | copy-start | bytes 98308
  127.5 1.2 copy-start.6
  213.8 16.4 %all-to-all-start.1 = ((bf16[8,128,256]{1,2,0:T(8,128)(2,1)}), bf16[8,128,256]{1,2,0:T(8,128)(2,1)}, u32[]{:S(2)}, u32[]{:S(2)}) async-start(bf16[8,128,256]{1,2,0:T(8,128)(2,1)} %broadcast_in_dim.36), calls=%async_computation.1 | async-start | bytes 1048576 | tf_op jit(solution)/shard_map/all_to_all | solution.py:20
  226.0 7.8 %copy-start.13 = (pred[3]{0:T(512)(128)(4,1)S(1)}, pred[3]{0:T(512)(128)(4,1)}, u32[]{:S(2)}) copy-start(pred[3]{0:T(512)(128)(4,1)} %compare_and_fusion.1) | copy-start | bytes 13
  226.0 9.6 %copy-start.9 = (bf16[1,2,128,128]{3,2,1,0:T(8,128)(2,1)S(1)}, bf16[1,2,128,128]{3,2,1,0:T(8,128)(2,1)}, u32[]{:S(2)}) copy-start(bf16[1,2,128,128]{3,2,1,0:T(8,128)(2,1)} %param.29) | copy-start | bytes 196612
  226.0 11.5 %copy-start.5 = (f32[256,1536]{0,1:T(8,128)S(1)}, f32[256,1536]{0,1:T(8,128)}, u32[]{:S(2)}) copy-start(f32[256,1536]{0,1:T(8,128)} %fusion.4) | copy-start | bytes 4718596
Sparse Core Ops, SparseCore 0:
  10.8 84.0 all-gather.2
  130.0 78.7 all-gather.4
where the time goes:
time: 254 us; the launch traced here: 251 us
  waiting for transfers between devices  159 us (63%)
  matrix products  38 us (15%)
  local copies, waits for them, and re-layouts  27.2 us (11%)
  between operations  13.7 us (5%)
  starting transfers between devices  8.66 us (3%)
  other arithmetic  4.61 us (2%)
    all_gather x2, waiting for transfers between devices, sent_together(): lax.all_gather(both, axis, axis=dim, tiled=True)  155 us
    dot_general x2, matrix products, apply_matrix(): jnp.dot(diag_blocks[0], vector, preferred_element_type=jnp.float32)  10.3 us
    all_to_all x2, starting transfers between devices, copy_for_each(): return lax.all_to_all(copies, axis, split_axis=0, concat_axis=0, tiled=True)  8.58 us
    dot_general x2, matrix products, smooth(): jnp.dot(precond[0], residual.astype(jnp.bfloat16), preferred_element_type...  8.51 us
    unnamed x31, local copies, waits for them, and re-layouts  6.49 us
    gather x2, local copies, waits for them, and re-layouts, far_field(): picked = jnp.take(sibling_coefs, slots, axis=0)  5.13 us
  transfers between devices with their start and end apart: 4, of which 3 were waited for; matrix products, arithmetic and copies ran while one was open for 10% of the time, Pallas kernels for 0%

commit v1 on v0

v1 whole, which is shorter than its diff:
```python
import functools

import jax
import jax.numpy as jnp
from jax import lax
from jax.experimental import pallas as pl
from jax.experimental.pallas import tpu as pltpu
from jax.sharding import PartitionSpec as P

damping = 0.7
MESH = pl.DeviceIdType.MESH
NY, NZ, NC = 4, 8, 8
F32, BF16 = jnp.float32, jnp.bfloat16


def dot_nn(a, b):
    return jnp.dot(a, b, preferred_element_type=F32)


def dot_nt(a, b):
    return lax.dot_general(a, b, (((1,), (1,)), ((), ())), preferred_element_type=F32)


def dot_tn(a, b):
    return lax.dot_general(a, b, (((0,), (0,)), ((), ())), preferred_element_type=F32)


def kernel(
    lists_ref,
    owner_ref,
    clist_ref,
    glist_ref,
    rhs_hbm,
    guess_hbm,
    diag_hbm,
    prec_hbm,
    bases_hbm,
    trans_hbm,
    mid_hbm,
    coup_hbm,
    ccoup_hbm,
    gcoup_hbm,
    out_ref,
    rhs,
    guess,
    diag,
    prec,
    bases,
    trans,
    mid,
    ccoup,
    gcoup,
    coup_all,
    meta_all,
    weights,
    mmat,
    emat,
    rnb,
    first,
    firsth,
    pb,
    gmat,
    w_t,
    acc,
    coef,
    uterm_send,
    uterm_recv,
    row_recv,
    cc_recv,
    ct_all,
    part_send,
    part_recv,
    load_sem,
    wt_send,
    wt_recv,
    ag_send,
    ag_recv,
    rs_send,
    rs_recv,
    ys_send,
    ys_recv,
    cx_send,
    cx_recv,
    ct_send,
    ct_recv,
    pt_send,
    pt_recv,
):
    top, mdl, leaf = lax.axis_index("top"), lax.axis_index("mid"), lax.axis_index("leaf")
    y, z = leaf // NZ, lax.rem(leaf, NZ)
    cluster = top * 2 + mdl
    n, cols = rhs.shape
    rank = bases.shape[1]
    piece = cols // NZ
    tile = n // 6

    def z_peer(dz):
        return (top, mdl, y * NZ + lax.rem(z + dz + NZ, NZ))

    def y_peer(dy):
        return (top, mdl, lax.rem(y + dy, NY) * NZ + z)

    def c_peer(dc):
        other = lax.rem(cluster + dc, NC)
        return (other // 2, lax.rem(other, 2), leaf)

    barrier = pltpu.get_barrier_semaphore()
    for dz in range(1, NZ):
        pl.semaphore_signal(barrier, inc=1, device_id=z_peer(dz), device_id_type=MESH)
    for dy in range(1, NY):
        pl.semaphore_signal(barrier, inc=1, device_id=y_peer(dy), device_id_type=MESH)
    for dc in range(1, NC):
        pl.semaphore_signal(barrier, inc=1, device_id=c_peer(dc), device_id_type=MESH)

    loads = {}
    for i, (name, src, dst) in enumerate(
        (
            ("guess", guess_hbm, guess),
            ("bases", bases_hbm.at[0], bases),
            ("trans", trans_hbm.at[0], trans),
            ("mid", mid_hbm, mid),
            ("ccoup", ccoup_hbm.at[0], ccoup),
            ("gcoup", gcoup_hbm.at[0], gcoup),
            ("coup", coup_hbm.at[0], coup_all.at[0]),
            ("rhs", rhs_hbm, rhs),
            ("diag", diag_hbm.at[0], diag),
            ("prec", prec_hbm.at[0], prec),
        )
    ):
        loads[name] = pltpu.make_async_copy(src, dst, load_sem.at[i])
        loads[name].start()

    sent = []

    def send(src, dst, send_sem, recv_sem, peer):
        copy = pltpu.make_async_remote_copy(
            src_ref=src,
            dst_ref=dst,
            send_sem=send_sem,
            recv_sem=recv_sem,
            device_id=peer,
            device_id_type=MESH,
        )
        copy.start()
        sent.append(copy)

    def arrived(dst, send_sem, recv_sem, peer):
        pltpu.make_async_remote_copy(
            src_ref=dst,
            dst_ref=dst,
            send_sem=send_sem,
            recv_sem=recv_sem,
            device_id=peer,
            device_id_type=MESH,
        ).wait_recv()

    rows = lax.broadcasted_iota(jnp.int32, (8, rank), 0)
    meta = jnp.zeros((8, rank), jnp.int32)
    for k in range(4):
        meta = jnp.where(rows == k, owner_ref[0, lists_ref[0, k]], meta)
    meta_all[0] = meta

    def start_exchange(r, coef_t):
        coef[r, 0] = coef_t
        loads["trans"].wait() if r == 0 else None
        uterm_send[r] = dot_nn(coef_t, trans[...]).astype(BF16)
        if r == 0:
            pl.semaphore_wait(barrier, 2 * (NZ - 1) + NY - 1)
        for dz in (4, 3, 5, 2, 6, 1, 7):
            there = lax.rem(z + dz, NZ)
            send(
                uterm_send.at[r, pl.ds(pl.multiple_of(there * piece, piece), piece)],
                uterm_recv.at[r, NZ - dz],
                rs_send.at[r, dz],
                rs_recv.at[r, NZ - dz],
                z_peer(dz),
            )
        for dz in (2, 6, 1, 7):
            send(
                coef.at[r, 0],
                coef.at[r, NZ - dz],
                ag_send.at[r, dz],
                ag_recv.at[r, NZ - dz],
                z_peer(dz),
            )

    half = cols // 2

    def relay(r):
        arrived(coef.at[r, 6], ag_send.at[r, 2], ag_recv.at[r, 6], z_peer(2))
        send(coef.at[r, 6, pl.ds(0, half)], coef.at[r, 4, pl.ds(0, half)], ag_send.at[r, 4], ag_recv.at[r, 4], z_peer(2))
        send(coef.at[r, 6], coef.at[r, 5], ag_send.at[r, 3], ag_recv.at[r, 5], z_peer(1))
        arrived(coef.at[r, 2], ag_send.at[r, 6], ag_recv.at[r, 2], z_peer(6))
        send(coef.at[r, 2, pl.ds(half, half)], coef.at[r, 4, pl.ds(half, half)], ag_send.at[r, 0], ag_recv.at[r, 0], z_peer(6))
        send(coef.at[r, 2], coef.at[r, 3], ag_send.at[r, 5], ag_recv.at[r, 3], z_peer(7))

    def row_sum(r):
        mine = pl.ds(pl.multiple_of(z * piece, piece), piece)
        total = uterm_send[r, mine].astype(F32)
        for k in range(1, NZ):
            arrived(uterm_recv.at[r, k], rs_send.at[r, NZ - k], rs_recv.at[r, k], z_peer(k))
            total = total + uterm_recv[r, k].astype(F32)
        row_recv[r, 0] = total.astype(BF16)
        for dy in (2, 1, 3):
            send(row_recv.at[r, 0], row_recv.at[r, NY - dy], ys_send.at[r, dy], ys_recv.at[r, NY - dy], y_peer(dy))

    def cluster_sum(r):
        total = row_recv[r, 0].astype(F32)
        for k in range(1, NY):
            arrived(row_recv.at[r, k], ys_send.at[r, NY - k], ys_recv.at[r, k], y_peer(k))
            total = total + row_recv[r, k].astype(F32)
        cc_recv[r, 0] = total.astype(BF16)
        for dc in range(1, NC):
            send(cc_recv.at[r, 0], cc_recv.at[r, NC - dc], cx_send.at[r, dc], cx_recv.at[r, NC - dc], c_peer(dc))

    def cluster_total(r):
        total = dot_nt(cc_recv[r, 0], mmat[0])
        for k in range(1, NC):
            arrived(cc_recv.at[r, k], cx_send.at[r, NC - k], cx_recv.at[r, k], c_peer(k))
            total = total + dot_nt(cc_recv[r, k], mmat[k])
        mine = pl.ds(pl.multiple_of(z * piece, piece), piece)
        ct_all[r, mine] = total.astype(BF16)
        for dz in (4, 3, 5, 2, 6, 1, 7):
            send(ct_all.at[r, mine], ct_all.at[r, mine], ct_send.at[r, dz], ct_recv.at[r, NZ - dz], z_peer(dz))

    def partial_sums(r):
        acc[...] = dot_nt(coef[r, 0], weights[0])
        for k in (2, 6):
            acc[...] += dot_nt(coef[r, k], weights[k])
        for k in (1, 7, 3, 5):
            arrived(coef.at[r, k], ag_send.at[r, NZ - k], ag_recv.at[r, k], z_peer(k))
            acc[...] += dot_nt(coef[r, k], weights[k])
        low, high = coef.at[r, 4, pl.ds(0, half)], coef.at[r, 4, pl.ds(half, half)]
        arrived(low, ag_send.at[r, 4], ag_recv.at[r, 4], z_peer(6))
        arrived(high, ag_send.at[r, 0], ag_recv.at[r, 0], z_peer(2))
        acc[...] += dot_nt(coef[r, 4], weights[4])
        for j in (2, 1, 3):
            part_send[r, j] = acc[:, j * rank : (j + 1) * rank].astype(BF16)
            send(part_send.at[r, j], part_recv.at[r, NY - j], pt_send.at[r, j], pt_recv.at[r, NY - j], y_peer(j))

    def leaf_total(r):
        total = acc[:, 0:rank]
        for k in range(1, NY):
            arrived(part_recv.at[r, k], pt_send.at[r, NY - k], pt_recv.at[r, k], y_peer(k))
            total = total + part_recv[r, k].astype(F32)
        for k in range(1, NZ):
            there = lax.rem(z + k, NZ)
            theirs = ct_all.at[r, pl.ds(pl.multiple_of(there * piece, piece), piece)]
            arrived(theirs, ct_send.at[r, NZ - k], ct_recv.at[r, k], z_peer(k))
        return (total + dot_nt(ct_all[r], trans[...])).astype(BF16)

    loads["guess"].wait()
    loads["bases"].wait()
    start_exchange(0, dot_tn(bases[...], guess[...]).T.astype(BF16))

    for dy in (2, 1, 3):
        send(meta_all.at[0], meta_all.at[NY - dy], wt_send.at[0, dy], wt_recv.at[0, NY - dy], y_peer(dy))
        send(coup_hbm.at[0], coup_all.at[NY - dy], wt_send.at[1, dy], wt_recv.at[1, NY - dy], y_peer(dy))

    loads["mid"].wait()
    loads["gcoup"].wait()
    loads["ccoup"].wait()
    for k in range(2):
        emat[k] = dot_nn(mid[cluster], gcoup[k])

    def compose(k, carry):
        other = lax.rem(cluster + k, NC)
        pick = jnp.zeros((rank, rank), F32)
        for i in range(2):
            pick = pick + jnp.where(glist_ref[0, i] == other // 2, 1.0, 0.0) * emat[i]
        value = dot_nt(pick.astype(BF16), mid[other])
        for i in range(3):
            value = value + jnp.where(clist_ref[0, i] == other, 1.0, 0.0) * ccoup[i].astype(F32)
        mmat[k] = value.astype(BF16)
        return carry

    lax.fori_loop(0, NC, compose, 0)

    loads["rhs"].wait()
    loads["diag"].wait()
    rnb[:, cols : cols + rank] = bases[...]

    def near(i, carry):
        at = pl.ds(pl.multiple_of(i * tile, tile), tile)
        rnb[at, 0:cols] = (rhs[at].astype(F32) - dot_nn(diag[at], guess[...])).astype(BF16)
        return carry

    lax.fori_loop(0, 6, near, 0)
    relay(0)
    row_sum(0)

    loads["prec"].wait()

    def smooth(i, carry):
        at = pl.ds(pl.multiple_of(i * tile, tile), tile)
        both = dot_nn(prec[at], rnb[...])
        base = guess[at].astype(F32) + damping * both[:, 0:cols]
        first[at] = base
        firsth[at] = base.astype(BF16)
        pb[at] = both[:, cols : cols + rank].astype(BF16)
        return carry

    lax.fori_loop(0, 6, smooth, 0)
    cluster_sum(0)

    loads["coup"].wait()
    for k in range(1, NY):
        arrived(meta_all.at[k], wt_send.at[0, NY - k], wt_recv.at[0, k], y_peer(k))
        arrived(coup_all.at[k], wt_send.at[1, NY - k], wt_recv.at[1, k], y_peer(k))

    def place(k, carry):
        slot = y * NZ + lax.rem(z + k, NZ)
        for j in range(NY):
            hit = jnp.where(meta_all[j] == slot, 1.0, 0.0)
            value = jnp.zeros((rank, rank), F32)
            for i in range(4):
                value = value + hit[i : i + 1] * coup_all[j, i].astype(F32)
            weights[k, j * rank : (j + 1) * rank] = value.astype(BF16)
        return carry

    lax.fori_loop(0, NZ, place, 0)
    gmat[...] = dot_tn(bases[...], pb[...]).astype(BF16)
    w_t[...] = dot_tn(bases[...], firsth[...]).T

    partial_sums(0)
    cluster_total(0)
    far = leaf_total(0)

    start_exchange(1, (w_t[...] - damping * dot_nt(far, gmat[...])).astype(BF16))

    def correct(i, carry):
        at = pl.ds(pl.multiple_of(i * tile, tile), tile)
        value = first[at] - damping * dot_nt(pb[at], far)
        first[at] = value
        firsth[at] = value.astype(BF16)
        return carry

    lax.fori_loop(0, 6, correct, 0)

    def near_again(i, carry):
        at = pl.ds(pl.multiple_of(i * tile, tile), tile)
        rnb[at, 0:cols] = (rhs[at].astype(F32) - dot_nn(diag[at], firsth[...])).astype(BF16)
        return carry

    lax.fori_loop(0, 6, near_again, 0)
    relay(1)
    row_sum(1)

    def smooth_again(i, carry):
        at = pl.ds(pl.multiple_of(i * tile, tile), tile)
        first[at] = first[at] + damping * dot_nn(prec[at], rnb[:, 0:cols])
        return carry

    lax.fori_loop(0, 6, smooth_again, 0)
    cluster_sum(1)
    partial_sums(1)
    cluster_total(1)
    far = leaf_total(1)

    def finish(i, carry):
        at = pl.ds(pl.multiple_of(i * tile, tile), tile)
        out_ref[at] = (first[at] - damping * dot_nt(pb[at], far)).astype(BF16)
        return carry

    lax.fori_loop(0, 6, finish, 0)
    for copy in sent:
        copy.wait_send()


def body(
    rhs,
    guess,
    diag_blocks,
    precond,
    bases,
    leaf_to_middle_transfer,
    mid_transfer,
    leaf_coupling,
    cluster_coupling,
    group_coupling,
    leaf_lists,
    owner,
    cluster_lists,
    group_lists,
):
    n, cols = rhs.shape
    rank = bases.shape[2]
    piece = cols // NZ
    smem = pl.BlockSpec(memory_space=pltpu.SMEM)
    hbm = pl.BlockSpec(memory_space=pl.ANY)
    dma = pltpu.SemaphoreType.DMA
    return pl.pallas_call(
        kernel,
        out_shape=jax.ShapeDtypeStruct((n, cols), BF16),
        in_specs=[smem] * 4 + [hbm] * 10,
        out_specs=pl.BlockSpec(memory_space=pltpu.VMEM),
        scratch_shapes=[
            pltpu.VMEM((n, cols), BF16),
            pltpu.VMEM((n, cols), BF16),
            pltpu.VMEM((n, n), BF16),
            pltpu.VMEM((n, n), BF16),
            pltpu.VMEM((n, rank), BF16),
            pltpu.VMEM((rank, rank), BF16),
            pltpu.VMEM((NC, rank, rank), BF16),
            pltpu.VMEM((3, rank, rank), BF16),
            pltpu.VMEM((2, rank, rank), BF16),
            pltpu.VMEM((NY, 4, rank, rank), BF16),
            pltpu.VMEM((NY, 8, rank), jnp.int32),
            pltpu.VMEM((NZ, NY * rank, rank), BF16),
            pltpu.VMEM((NC, rank, rank), BF16),
            pltpu.VMEM((2, rank, rank), F32),
            pltpu.VMEM((n, cols + rank), BF16),
            pltpu.VMEM((n, cols), F32),
            pltpu.VMEM((n, cols), BF16),
            pltpu.VMEM((n, rank), BF16),
            pltpu.VMEM((rank, rank), BF16),
            pltpu.VMEM((cols, rank), F32),
            pltpu.VMEM((cols, NY * rank), F32),
            pltpu.VMEM((2, NZ, cols, rank), BF16),
            pltpu.VMEM((2, cols, rank), BF16),
            pltpu.VMEM((2, NZ, piece, rank), BF16),
            pltpu.VMEM((2, NY, piece, rank), BF16),
            pltpu.VMEM((2, NC, piece, rank), BF16),
            pltpu.VMEM((2, cols, rank), BF16),
            pltpu.VMEM((2, NY, cols, rank), BF16),
            pltpu.VMEM((2, NY, cols, rank), BF16),
            dma((10,)),
            dma((2, NY)),
            dma((2, NY)),
            dma((2, NZ)),
            dma((2, NZ)),
            dma((2, NZ)),
            dma((2, NZ)),
            dma((2, NY)),
            dma((2, NY)),
            dma((2, NC)),
            dma((2, NC)),
            dma((2, NZ)),
            dma((2, NZ)),
            dma((2, NY)),
            dma((2, NY)),
        ],
        compiler_params=pltpu.CompilerParams(
            collective_id=0, has_side_effects=True, vmem_limit_bytes=60 * 1024 * 1024
        ),
    )(
        leaf_lists,
        owner,
        cluster_lists,
        group_lists,
        rhs,
        guess,
        diag_blocks,
        precond,
        bases,
        leaf_to_middle_transfer,
        mid_transfer,
        leaf_coupling,
        cluster_coupling,
        group_coupling,
    )


def solution(mesh):
    in_specs = (
        P(("top", "mid", "leaf"), None),
        P(("top", "mid", "leaf"), None),
        P(("top", "mid", "leaf"), None, None),
        P(("top", "mid", "leaf"), None, None),
        P(("top", "mid", "leaf"), None, None),
        P(("top", "mid", "leaf"), None, None),
        P(),
        P(("top", "mid", "leaf"), None, None, None),
        P(("top", "mid"), None, None, None),
        P("top", None, None, None),
        P(("top", "mid", "leaf"), None),
        P(("top", "mid"), None),
        P(("top", "mid"), None),
        P("top", None),
    )
    out_specs = P(("top", "mid", "leaf"), None)
    return jax.shard_map(body, mesh=mesh, in_specs=in_specs, out_specs=out_specs, check_vma=False)
```

time: 254 us -> 54.8 us (0.22)
  waiting for transfers between devices: 159 us -> 0 us
  Pallas kernels: 0 us -> 51.8 us
  matrix products: 38 us -> 0 us
  local copies, waits for them, and re-layouts: 27.2 us -> 2.06 us
  between operations: 13.7 us -> 0.01 us
  starting transfers between devices: 8.66 us -> 0 us
  other arithmetic: 4.61 us -> 0 us
    all_gather x2 -> x0, waiting for transfers between devices: 155 us -> none  [sent_together(): lax.all_gather(both, axis, axis=dim, tiled=True)]
    pallas_call x0 -> x1, Pallas kernels: none -> 51.8 us  [body(): pl.pallas_call(kernel, out_shape=jax.ShapeDtypeStruct((n, cols), BF16), i...]
    dot_general x18 -> x0, matrix products: 38 us -> none  [the longest x2 10.3 us: apply_matrix(): jnp.dot(diag_blocks[0], vector, preferred_element_type=jnp.float32)]
    gather x7 -> x0, local copies, waits for them, and re-layouts: 11.4 us -> none  [the longest x2 5.13 us: far_field(): picked = jnp.take(sibling_coefs, slots, axis=0)]
    all_to_all x2 -> x0, starting transfers between devices: 8.58 us -> none  [copy_for_each(): return lax.all_to_all(copies, axis, split_axis=0, concat_axis=0, tiled=True)]
    unnamed x31 -> x1, local copies, waits for them, and re-layouts: 6.49 us -> 2.06 us
    all_to_all x2 -> x0, waiting for transfers between devices: 3.91 us -> none  [copy_for_each(): return lax.all_to_all(copies, axis, split_axis=0, concat_axis=0, tiled=True)]
    split x1 -> x0, local copies, waits for them, and re-layouts: 3.83 us -> none  [sent_together(): jnp.split(lax.all_gather(both, axis, axis=dim, tiled=True), ends, axis=al...]
  transfers between devices with their start and end apart: 4 -> 0, of which waited for: 3 -> 0; matrix products, arithmetic and copies ran while one was open for 10% -> 0% of each run, Pallas kernels for 0% -> 0%
where the time goes in v1:
time: 54.8 us; the launch traced here: 53.9 us
  Pallas kernels  51.8 us (95%)
  local copies, waits for them, and re-layouts  2.06 us (4%)
    pallas_call x1, Pallas kernels, body(): pl.pallas_call(kernel, out_shape=jax.ShapeDtypeStruct((n, cols), BF16), i...  51.8 us
    unnamed x1, local copies, waits for them, and re-layouts  2.06 us

profile of v1, /device:TPU:32, one launch (start us, length us, event | category | flops | bytes accessed | tf_op | source)
XLA Modules:
  0.0 53.9 jit_solution(9102845725295553926)
XLA Ops:
  0.0 51.8 %shard_map.136 = bf16[1536,256]{1,0:T(8,128)(2,1)} custom-call(s32[1,4]{1,0:T(1,128)} %lists_ref.1, s32[1,32]{1,0:T(1,128)} %owner_ref.1, s32[1,3]{1,0:T(1,128)} %clist_ref.1, s32[1,2]{1,0:T(1,128)} %glist_ref.1, bf16[1536,256]{1,0:T(8,128)(2,1)} %rhs_hbm.1, bf16[1536,256]{1,0:T(8,128)(2,1)} %guess_hbm.1, bf16[1,1536,1536]{2,1,0:T(8,128)(2,1)} %diag_hbm.1, ...), custom_call_target="tpu_custom_call" | custom-call | tf_op jit(solution)/shard_map/pallas_call | solution.py:392
  51.8 2.1 %copy.16 = bf16[1536,256]{1,0:T(8,128)(2,1)} copy(bf16[1536,256]{1,0:T(8,128)(2,1)} %shard_map.136) | data formatting | bytes 1572864

commit v2 on v1

v2 whole, which is shorter than its diff:
```python
import jax
import jax.numpy as jnp
from jax import lax
from jax.experimental import pallas as pl
from jax.experimental.pallas import tpu as pltpu
from jax.sharding import PartitionSpec as P

damping = 0.7
MESH = pl.DeviceIdType.MESH
NY, NZ, NC = 4, 8, 8
TILES = 3
ABROAD = [(dc, dy) for dc in range(NC) for dy in range(NY) if dc or dy]
COLUMN = [(0, 2), (0, 1), (0, 3)]
PLACE = {0: 0, 1: 1, 7: 2, 2: 3, 6: 4, 3: 5, 5: 6, 4: 7}
F32, BF16 = jnp.float32, jnp.bfloat16


def dot_nn(a, b):
    return jnp.dot(a, b, preferred_element_type=F32)


def dot_nt(a, b):
    return lax.dot_general(a, b, (((1,), (1,)), ((), ())), preferred_element_type=F32)


def dot_tn(a, b):
    return lax.dot_general(a, b, (((0,), (0,)), ((), ())), preferred_element_type=F32)


def kernel(
    lists_hbm,
    owner_hbm,
    clist_hbm,
    glist_hbm,
    rhs_hbm,
    guess_hbm,
    diag_hbm,
    prec_hbm,
    bases_hbm,
    trans_hbm,
    mid_hbm,
    coup_hbm,
    ccoup_hbm,
    gcoup_hbm,
    out_ref,
    lists_ref,
    owner_ref,
    clist_ref,
    glist_ref,
    rhs,
    guess,
    diag,
    prec,
    bases,
    trans,
    mid,
    ccoup,
    gcoup,
    coup_all,
    meta_all,
    weights,
    mmat,
    emat,
    rnb,
    first,
    firsth,
    pb,
    gmat,
    w_t,
    acc,
    coef,
    uterm_send,
    uterm_recv,
    row_recv,
    cc_all,
    ct_all,
    part_send,
    part_recv,
    load_sem,
    wt_send,
    wt_recv,
    ag_send,
    ag_recv,
    rs_send,
    rs_recv,
    ys_send,
    ys_recv,
    cx_send,
    cx_recv,
    ct_send,
    ct_recv,
    pt_send,
    pt_recv,
):
    top, mdl, leaf = lax.axis_index("top"), lax.axis_index("mid"), lax.axis_index("leaf")
    y, z = leaf // NZ, lax.rem(leaf, NZ)
    cluster = top * 2 + mdl
    n, cols = rhs.shape
    rank = bases.shape[1]
    piece = cols // NZ
    half = cols // 2
    tile = n // TILES

    def z_peer(dz):
        return (top, mdl, y * NZ + lax.rem(z + dz, NZ))

    def y_peer(dy):
        return (top, mdl, lax.rem(y + dy, NY) * NZ + z)

    def c_peer(dc, dy):
        other = lax.rem(cluster + dc, NC)
        return (other // 2, lax.rem(other, 2), lax.rem(y + dy, NY) * NZ + z)

    loads = {}
    for i, (name, src, dst) in enumerate(
        (
            ("guess", guess_hbm, guess),
            ("bases", bases_hbm.at[0], bases),
            ("trans", trans_hbm.at[0], trans),
            ("lists", lists_hbm, lists_ref),
            ("owner", owner_hbm, owner_ref),
            ("clist", clist_hbm, clist_ref),
            ("glist", glist_hbm, glist_ref),
            ("rhs", rhs_hbm, rhs),
            ("diag", diag_hbm.at[0], diag),
            ("mid", mid_hbm, mid),
            ("ccoup", ccoup_hbm.at[0], ccoup),
            ("gcoup", gcoup_hbm.at[0], gcoup),
            ("coup", coup_hbm.at[0], coup_all.at[0]),
            ("prec", prec_hbm.at[0], prec),
        )
    ):
        loads[name] = pltpu.make_async_copy(src, dst, load_sem.at[i])
        loads[name].start()

    barrier = pltpu.get_barrier_semaphore()
    for dz in (4, 3, 5, 2, 6, 1, 7):
        pl.semaphore_signal(barrier, inc=1, device_id=z_peer(dz), device_id_type=MESH)
    for dc, dy in ABROAD:
        pl.semaphore_signal(barrier, inc=1, device_id=c_peer(dc, dy), device_id_type=MESH)

    def send(src, dst, send_sem, recv_sem, peer):
        copy = pltpu.make_async_remote_copy(
            src_ref=src,
            dst_ref=dst,
            send_sem=send_sem,
            recv_sem=recv_sem,
            device_id=peer,
            device_id_type=MESH,
        )
        copy.start()

    def arrived(dst, send_sem, recv_sem):
        pltpu.make_async_remote_copy(
            src_ref=dst,
            dst_ref=dst,
            send_sem=send_sem,
            recv_sem=recv_sem,
            device_id=z_peer(1),
            device_id_type=MESH,
        ).wait_recv()

    def left(src, send_sem, recv_sem):
        pltpu.make_async_remote_copy(
            src_ref=src,
            dst_ref=src,
            send_sem=send_sem,
            recv_sem=recv_sem,
            device_id=z_peer(1),
            device_id_type=MESH,
        ).wait_send()

    mine = pl.ds(pl.multiple_of(z * piece, piece), piece)

    def block(r, h, k):
        return coef.at[r, pl.ds(h * half, half), pl.ds(PLACE[k] * rank, rank)]

    def pass_on(r, h, source, k, dz):
        send(block(r, h, source), block(r, h, k), ag_send.at[r], ag_recv.at[r, h, k], z_peer(dz))

    def here(r, h, k):
        arrived(block(r, h, k), ag_send.at[r], ag_recv.at[r, h, k])

    def start_exchange(r, coef_t):
        coef[r, :, 0:rank] = coef_t
        if r == 0:
            loads["trans"].wait()
        uterm_send[r] = dot_nn(coef_t, trans[...]).astype(BF16)
        if r == 0:
            pl.semaphore_wait(barrier, NZ - 1 + len(ABROAD))
        for dz in (4, 3, 5, 2, 6, 1, 7):
            there = lax.rem(z + dz, NZ)
            send(
                uterm_send.at[r, pl.ds(pl.multiple_of(there * piece, piece), piece)],
                uterm_recv.at[r, NZ - dz],
                rs_send.at[r],
                rs_recv.at[r],
                z_peer(dz),
            )
        for dz in (2, 6, 1, 7):
            for h in range(2):
                pass_on(r, h, 0, NZ - dz, dz)

    def relay(r, h):
        here(r, h, 6)
        if h == 0:
            pass_on(r, h, 6, 4, 2)
        pass_on(r, h, 6, 5, 1)
        here(r, h, 2)
        if h == 1:
            pass_on(r, h, 2, 4, 6)
        pass_on(r, h, 2, 3, 7)

    def row_sum(r):
        arrived(uterm_recv.at[r, pl.ds(1, NZ - 1)], rs_send.at[r], rs_recv.at[r])
        total = uterm_send[r, mine].astype(F32)
        for k in range(1, NZ):
            total = total + uterm_recv[r, k].astype(F32)
        row_recv[r, 0] = total.astype(BF16)
        for dc, dy in ABROAD if r else COLUMN:
            k = (NC - dc) % NC * NY + (NY - dy) % NY
            send(row_recv.at[r, 0], row_recv.at[r, k], ys_send.at[r], ys_recv.at[r], c_peer(dc, dy))

    def cluster_sum(r, k):
        total = row_recv[r, k * NY].astype(F32)
        for dy in range(1, NY):
            total = total + row_recv[r, k * NY + dy].astype(F32)
        cc_all[r, :, k * rank : (k + 1) * rank] = total.astype(BF16)

    def pass_sum():
        arrived(row_recv.at[0, pl.ds(1, NY - 1)], ys_send.at[0], ys_recv.at[0])
        cluster_sum(0, 0)
        for dc in range(1, NC):
            there = cc_all.at[0, :, pl.ds((NC - dc) * rank, rank)]
            send(cc_all.at[0, :, pl.ds(0, rank)], there, cx_send, cx_recv, c_peer(dc, 0))

    def cluster_total(r):
        if r == 0:
            arrived(cc_all.at[0, :, pl.ds(rank, (NC - 1) * rank)], cx_send, cx_recv)
        else:
            arrived(row_recv.at[r, pl.ds(1, NC * NY - 1)], ys_send.at[r], ys_recv.at[r])
            for k in range(NC):
                cluster_sum(r, k)
        ct_all[r, mine] = dot_nt(cc_all[r], mmat[...]).astype(BF16)
        for dz in (4, 3, 5, 2, 6, 1, 7):
            send(ct_all.at[r, mine], ct_all.at[r, mine], ct_send.at[r], ct_recv.at[r], z_peer(dz))

    def early_sums(r):
        for h in range(2):
            here(r, h, 1)
            here(r, h, 7)
        acc[...] = dot_nt(coef[r, :, 0 : 5 * rank], weights[:, 0 : 5 * rank])

    def late_sums(r, h):
        for k in (3, 5, 4):
            here(r, h, k)
        rows = slice(h * half, (h + 1) * half)
        value = acc[rows] + dot_nt(coef[r, rows, 5 * rank :], weights[:, 5 * rank :])
        acc[rows, 0:rank] = value[:, 0:rank]
        for j in (2, 1, 3):
            part_send[r, j, rows] = value[:, j * rank : (j + 1) * rank].astype(BF16)
        for j in (2, 1, 3):
            send(
                part_send.at[r, j, pl.ds(h * half, half)],
                part_recv.at[r, h, NY - j],
                pt_send.at[r],
                pt_recv.at[r, h],
                y_peer(j),
            )

    def leaf_total(r):
        for h in range(2):
            arrived(part_recv.at[r, h, pl.ds(1, NY - 1)], pt_send.at[r], pt_recv.at[r, h])
        totals = []
        for h in range(2):
            total = acc[h * half : (h + 1) * half, 0:rank]
            for k in range(1, NY):
                total = total + part_recv[r, h, k].astype(F32)
            totals.append(total)
        total = jnp.concatenate(totals, axis=0)
        arrived(ct_all.at[r, pl.ds(0, cols - piece)], ct_send.at[r], ct_recv.at[r])
        return (total + dot_nt(ct_all[r], trans[...])).astype(BF16)

    def all_left(r):
        left(uterm_send.at[r, pl.ds(0, cols - piece)], rs_send.at[r], rs_recv.at[r])
        left(coef.at[r, :, pl.ds(0, 7 * rank)], ag_send.at[r], ag_recv.at[r, 0, 0])
        if r == 0:
            left(row_recv.at[r, pl.ds(1, NY - 1)], ys_send.at[r], ys_recv.at[r])
            left(cc_all.at[r, :, pl.ds(rank, (NC - 1) * rank)], cx_send, cx_recv)
        else:
            left(row_recv.at[r, pl.ds(1, NC * NY - 1)], ys_send.at[r], ys_recv.at[r])
        left(ct_all.at[r, pl.ds(0, cols - piece)], ct_send.at[r], ct_recv.at[r])
        left(part_send.at[r, pl.ds(1, NY - 1)], pt_send.at[r], pt_recv.at[r, 0])

    def tiles(step, begin=0, end=TILES):
        def run(i, carry):
            step(pl.ds(pl.multiple_of(i * tile, tile), tile))
            return carry

        lax.fori_loop(begin, end, run, 0)

    loads["guess"].wait()
    loads["bases"].wait()
    start_exchange(0, dot_tn(bases[...], guess[...]).T.astype(BF16))

    loads["lists"].wait()
    loads["owner"].wait()
    rows = lax.broadcasted_iota(jnp.int32, (8, rank), 0)
    meta = jnp.zeros((8, rank), jnp.int32)
    for k in range(4):
        meta = jnp.where(rows == k, owner_ref[0, lists_ref[0, k]], meta)
    meta_all[0] = meta
    for dy in (2, 1, 3):
        send(coup_hbm.at[0], coup_all.at[NY - dy], wt_send.at[1], wt_recv.at[1], y_peer(dy))
        send(meta_all.at[0], meta_all.at[NY - dy], wt_send.at[0], wt_recv.at[0], y_peer(dy))

    loads["rhs"].wait()
    loads["diag"].wait()
    rnb[:, cols : cols + rank] = bases[...]

    def near(at):
        rnb[at, 0:cols] = (rhs[at].astype(F32) - dot_nn(diag[at], guess[...])).astype(BF16)

    tiles(near)

    for name in ("mid", "gcoup", "ccoup", "clist", "glist"):
        loads[name].wait()
    for k in range(2):
        emat[k] = dot_nn(mid[cluster], gcoup[k])

    def compose(k, carry):
        other = lax.rem(cluster + k, NC)
        pick = jnp.zeros((rank, rank), F32)
        for i in range(2):
            pick = pick + jnp.where(glist_ref[0, i] == other // 2, 1.0, 0.0) * emat[i]
        value = dot_nt(pick.astype(BF16), mid[other])
        for i in range(3):
            value = value + jnp.where(clist_ref[0, i] == other, 1.0, 0.0) * ccoup[i].astype(F32)
        mmat[:, pl.ds(pl.multiple_of(k * rank, rank), rank)] = value.astype(BF16)
        return carry

    lax.fori_loop(0, NC, compose, 0)

    row_sum(0)
    relay(0, 0)
    relay(0, 1)

    loads["prec"].wait()

    def smooth(at):
        both = dot_nn(prec[at], rnb[...])
        base = guess[at].astype(F32) + damping * both[:, 0:cols]
        first[at] = base
        firsth[at] = base.astype(BF16)
        pb[at] = both[:, cols : cols + rank].astype(BF16)

    tiles(smooth, 0, 1)
    pass_sum()

    loads["coup"].wait()
    arrived(meta_all.at[pl.ds(1, NY - 1)], wt_send.at[0], wt_recv.at[0])
    arrived(coup_all.at[pl.ds(1, NY - 1)], wt_send.at[1], wt_recv.at[1])

    def place(p, carry):
        away = ((p + 1) // 2) * (2 * lax.rem(p, 2) - 1)
        slot = y * NZ + lax.rem(z + away + NZ, NZ)
        for j in range(NY):
            hit = jnp.where(meta_all[j] == slot, 1.0, 0.0)
            value = jnp.zeros((rank, rank), F32)
            for i in range(4):
                value = value + hit[i : i + 1] * coup_all[j, i].astype(F32)
            weights[j * rank : (j + 1) * rank, pl.ds(pl.multiple_of(p * rank, rank), rank)] = value.astype(BF16)
        return carry

    lax.fori_loop(0, NZ, place, 0)
    early_sums(0)
    tiles(smooth, 1, 2)
    late_sums(0, 0)
    late_sums(0, 1)
    cluster_total(0)
    tiles(smooth, 2, 3)
    gmat[...] = dot_tn(bases[...], pb[...]).astype(BF16)
    w_t[...] = dot_tn(bases[...], firsth[...]).T
    far = leaf_total(0)

    start_exchange(1, (w_t[...] - damping * dot_nt(far, gmat[...])).astype(BF16))

    def correct(at):
        value = first[at] - damping * dot_nt(pb[at], far)
        first[at] = value
        firsth[at] = value.astype(BF16)

    correct(slice(0, n))

    def near_again(at):
        rnb[at, 0:cols] = (rhs[at].astype(F32) - dot_nn(diag[at], firsth[...])).astype(BF16)

    tiles(near_again)
    row_sum(1)
    relay(1, 0)
    relay(1, 1)

    def smooth_again(at):
        first[at] = first[at] + damping * dot_nn(prec[at], rnb[:, 0:cols])

    tiles(smooth_again)
    early_sums(1)
    late_sums(1, 0)
    late_sums(1, 1)
    cluster_total(1)
    all_left(0)
    left(meta_all.at[pl.ds(1, NY - 1)], wt_send.at[0], wt_recv.at[0])
    left(coup_all.at[pl.ds(1, NY - 1)], wt_send.at[1], wt_recv.at[1])
    far = leaf_total(1)

    def finish(at):
        out_ref[at] = (first[at] - damping * dot_nt(pb[at], far)).astype(BF16)

    finish(slice(0, n))
    all_left(1)


def body(
    rhs,
    guess,
    diag_blocks,
    precond,
    bases,
    leaf_to_middle_transfer,
    mid_transfer,
    leaf_coupling,
    cluster_coupling,
    group_coupling,
    leaf_lists,
    owner,
    cluster_lists,
    group_lists,
):
    n, cols = rhs.shape
    rank = bases.shape[2]
    piece = cols // NZ
    hbm = pl.BlockSpec(memory_space=pltpu.HBM)
    dma = pltpu.SemaphoreType.DMA
    return pl.pallas_call(
        kernel,
        out_shape=pltpu.VMEM((n, cols), BF16),
        in_specs=[hbm] * 14,
        out_specs=pl.BlockSpec(memory_space=pltpu.VMEM),
        scratch_shapes=[
            pltpu.SMEM(leaf_lists.shape, jnp.int32),
            pltpu.SMEM(owner.shape, jnp.int32),
            pltpu.SMEM(cluster_lists.shape, jnp.int32),
            pltpu.SMEM(group_lists.shape, jnp.int32),
            pltpu.VMEM((n, cols), BF16),
            pltpu.VMEM((n, cols), BF16),
            pltpu.VMEM((n, n), BF16),
            pltpu.VMEM((n, n), BF16),
            pltpu.VMEM((n, rank), BF16),
            pltpu.VMEM((rank, rank), BF16),
            pltpu.VMEM((NC, rank, rank), BF16),
            pltpu.VMEM((3, rank, rank), BF16),
            pltpu.VMEM((2, rank, rank), BF16),
            pltpu.VMEM((NY, 4, rank, rank), BF16),
            pltpu.VMEM((NY, 8, rank), jnp.int32),
            pltpu.VMEM((NY * rank, NZ * rank), BF16),
            pltpu.VMEM((rank, NC * rank), BF16),
            pltpu.VMEM((2, rank, rank), F32),
            pltpu.VMEM((n, cols + rank), BF16),
            pltpu.VMEM((n, cols), F32),
            pltpu.VMEM((n, cols), BF16),
            pltpu.VMEM((n, rank), BF16),
            pltpu.VMEM((rank, rank), BF16),
            pltpu.VMEM((cols, rank), F32),
            pltpu.VMEM((cols, NY * rank), F32),
            pltpu.VMEM((2, cols, NZ * rank), BF16),
            pltpu.VMEM((2, cols, rank), BF16),
            pltpu.VMEM((2, NZ, piece, rank), BF16),
            pltpu.VMEM((2, NC * NY, piece, rank), BF16),
            pltpu.VMEM((2, piece, NC * rank), BF16),
            pltpu.VMEM((2, cols, rank), BF16),
            pltpu.VMEM((2, NY, cols, rank), BF16),
            pltpu.VMEM((2, 2, NY, cols // 2, rank), BF16),
            dma((14,)),
            dma((2,)),
            dma((2,)),
            dma((2,)),
            dma((2, 2, NZ)),
            dma((2,)),
            dma((2,)),
            dma((2,)),
            dma((2,)),
            dma,
            dma,
            dma((2,)),
            dma((2,)),
            dma((2,)),
            dma((2, 2)),
        ],
        compiler_params=pltpu.CompilerParams(
            collective_id=0, has_side_effects=True, vmem_limit_bytes=67043328 - n * cols * 2
        ),
    )(
        leaf_lists,
        owner,
        cluster_lists,
        group_lists,
        rhs,
        guess,
        diag_blocks,
        precond,
        bases,
        leaf_to_middle_transfer,
        mid_transfer,
        leaf_coupling,
        cluster_coupling,
        group_coupling,
    )


def solution(mesh):
    in_specs = (
        P(("top", "mid", "leaf"), None),
        P(("top", "mid", "leaf"), None),
        P(("top", "mid", "leaf"), None, None),
        P(("top", "mid", "leaf"), None, None),
        P(("top", "mid", "leaf"), None, None),
        P(("top", "mid", "leaf"), None, None),
        P(),
        P(("top", "mid", "leaf"), None, None, None),
        P(("top", "mid"), None, None, None),
        P("top", None, None, None),
        P(("top", "mid", "leaf"), None),
        P(("top", "mid"), None),
        P(("top", "mid"), None),
        P("top", None),
    )
    out_specs = P(("top", "mid", "leaf"), None)
    return jax.shard_map(body, mesh=mesh, in_specs=in_specs, out_specs=out_specs, check_vma=False)
```

time: 54.8 us -> 45.5 us (0.83)
  Pallas kernels: 51.8 us -> 43.9 us
  local copies, waits for them, and re-layouts: 2.06 us -> 0.88 us
    pallas_call x1, Pallas kernels: 51.8 us -> 43.9 us  [body(): pl.pallas_call(kernel, out_shape=pltpu.VMEM((n, cols), BF16), in_specs=[h...]
    unnamed x1, local copies, waits for them, and re-layouts: 2.06 us -> 0.88 us
where the time goes in v2:
time: 45.5 us; the launch traced here: 44.8 us
  Pallas kernels  43.9 us (96%)
  local copies, waits for them, and re-layouts  0.88 us (2%)
    pallas_call x1, Pallas kernels, body(): pl.pallas_call(kernel, out_shape=pltpu.VMEM((n, cols), BF16), in_specs=[h...  43.9 us

profile of v2, /device:TPU:32, one launch (start us, length us, event | category | flops | bytes accessed | tf_op | source)
XLA Modules:
  0.0 44.8 jit_solution(13141023567260840935)
XLA Ops:
  0.0 43.9 %shard_map.136 = bf16[1536,256]{1,0:T(8,128)(2,1)S(1)} custom-call(s32[1,4]{1,0:T(1,128)} %lists_hbm.1, s32[1,32]{1,0:T(1,128)} %owner_hbm.1, s32[1,3]{1,0:T(1,128)} %clist_hbm.1, s32[1,2]{1,0:T(1,128)} %glist_hbm.1, bf16[1536,256]{1,0:T(8,128)(2,1)} %rhs_hbm.1, bf16[1536,256]{1,0:T(8,128)(2,1)} %guess_hbm.1, bf16[1,1536,1536]{2,1,0:T(8,128)(2,1)} %diag_hbm.1, ...), custom_call_target="tpu_custom_call" | custom-call | tf_op jit(solution)/shard_map/pallas_call | solution.py:444
  43.9 0.9 %copy.16 = bf16[1536,256]{1,0:T(8,128)(2,1)} copy(bf16[1536,256]{1,0:T(8,128)(2,1)S(1)} %shard_map.136) | data formatting | bytes 1572864

commit v3 on v2

--- a/solution.py
+++ b/solution.py
@@ -9,8 +9,8 @@
 MESH = pl.DeviceIdType.MESH
 NY, NZ, NC = 4, 8, 8
 TILES = 3
-ABROAD = [(dc, dy) for dc in range(NC) for dy in range(NY) if dc or dy]
-COLUMN = [(0, 2), (0, 1), (0, 3)]
+ABROAD = [(k, dy) for k in range(NC) for dy in range(NY) if k or dy]
+ABROAD.sort(key=lambda p: -((0, 2, 0, 2, 1, 1, 1, 1)[p[0]] + (0, 1, 2, 1)[p[1]]))
 PLACE = {0: 0, 1: 1, 7: 2, 2: 3, 6: 4, 3: 5, 5: 6, 4: 7}
 F32, BF16 = jnp.float32, jnp.bfloat16
 
@@ -51,7 +51,6 @@
     guess,
     diag,
     prec,
-    bases,
     trans,
     mid,
     ccoup,
@@ -64,7 +63,7 @@
     rnb,
     first,
     firsth,
-    pb,
+    pbx,
     gmat,
     w_t,
     acc,
@@ -73,7 +72,7 @@
     uterm_recv,
     row_recv,
     cc_all,
-    ct_all,
+    far,
     part_send,
     part_recv,
     load_sem,
@@ -96,7 +95,7 @@
     y, z = leaf // NZ, lax.rem(leaf, NZ)
     cluster = top * 2 + mdl
     n, cols = rhs.shape
-    rank = bases.shape[1]
+    rank = trans.shape[1]
     piece = cols // NZ
     half = cols // 2
     tile = n // TILES
@@ -107,16 +106,26 @@
     def y_peer(dy):
         return (top, mdl, lax.rem(y + dy, NY) * NZ + z)
 
-    def c_peer(dc, dy):
-        other = lax.rem(cluster + dc, NC)
-        return (other // 2, lax.rem(other, 2), lax.rem(y + dy, NY) * NZ + z)
+    def flipped(k):
+        high = lax.rem(top // 2 + k // 4, 2)
+        low = lax.rem(lax.rem(top, 2) + k // 2 % 2, 2)
+        return high * 2 + low, lax.rem(mdl + k % 2, 2)
+
+    def c_peer(k, dy):
+        return (*flipped(k), lax.rem(y + dy, NY) * NZ + z)
+
+    barrier = pltpu.get_barrier_semaphore()
+    for dz in (4, 3, 5, 2, 6, 1, 7):
+        pl.semaphore_signal(barrier, inc=1, device_id=z_peer(dz), device_id_type=MESH)
+    for dc, dy in ABROAD:
+        pl.semaphore_signal(barrier, inc=1, device_id=c_peer(dc, dy), device_id_type=MESH)
 
     loads = {}
     for i, (name, src, dst) in enumerate(
         (
+            ("bases", bases_hbm.at[0], rnb.at[:, pl.ds(0, rank)]),
+            ("trans", trans_hbm.at[0], trans),
             ("guess", guess_hbm, guess),
-            ("bases", bases_hbm.at[0], bases),
-            ("trans", trans_hbm.at[0], trans),
             ("lists", lists_hbm, lists_ref),
             ("owner", owner_hbm, owner_ref),
             ("clist", clist_hbm, clist_ref),
@@ -133,12 +142,6 @@
         loads[name] = pltpu.make_async_copy(src, dst, load_sem.at[i])
         loads[name].start()
 
-    barrier = pltpu.get_barrier_semaphore()
-    for dz in (4, 3, 5, 2, 6, 1, 7):
-        pl.semaphore_signal(barrier, inc=1, device_id=z_peer(dz), device_id_type=MESH)
-    for dc, dy in ABROAD:
-        pl.semaphore_signal(barrier, inc=1, device_id=c_peer(dc, dy), device_id_type=MESH)
-
     def send(src, dst, send_sem, recv_sem, peer):
         copy = pltpu.make_async_remote_copy(
             src_ref=src,
@@ -181,11 +184,9 @@
     def here(r, h, k):
         arrived(block(r, h, k), ag_send.at[r], ag_recv.at[r, h, k])
 
-    def start_exchange(r, coef_t):
-        coef[r, :, 0:rank] = coef_t
-        if r == 0:
-            loads["trans"].wait()
-        uterm_send[r] = dot_nn(coef_t, trans[...]).astype(BF16)
+    def start_exchange(r, both):
+        coef[r, :, 0:rank] = both[:, 0:rank].astype(BF16)
+        uterm_send[r] = both[:, rank:].astype(BF16)
         if r == 0:
             pl.semaphore_wait(barrier, NZ - 1 + len(ABROAD))
         for dz in (4, 3, 5, 2, 6, 1, 7):
@@ -216,34 +217,42 @@
         total = uterm_send[r, mine].astype(F32)
         for k in range(1, NZ):
             total = total + uterm_recv[r, k].astype(F32)
-        row_recv[r, 0] = total.astype(BF16)
-        for dc, dy in ABROAD if r else COLUMN:
-            k = (NC - dc) % NC * NY + (NY - dy) % NY
-            send(row_recv.at[r, 0], row_recv.at[r, k], ys_send.at[r], ys_recv.at[r], c_peer(dc, dy))
-
-    def cluster_sum(r, k):
+        if r == 0:
+            cc_all[0, :, 0:rank] = total.astype(BF16)
+            for k in (1, 3, 4, 5, 6, 7, 2):
+                there = cc_all.at[0, :, pl.ds(k * rank, rank)]
+                send(cc_all.at[0, :, pl.ds(0, rank)], there, cx_send, cx_recv, c_peer(k, 0))
+        else:
+            row_recv[1, 0] = total.astype(BF16)
+            for k, dy in ABROAD:
+                there = row_recv.at[1, k * NY + (NY - dy) % NY]
+                send(row_recv.at[1, 0], there, ys_send.at[1], ys_recv.at[1], c_peer(k, dy))
+
+    def column_sum(r, k):
         total = row_recv[r, k * NY].astype(F32)
         for dy in range(1, NY):
             total = total + row_recv[r, k * NY + dy].astype(F32)
-        cc_all[r, :, k * rank : (k + 1) * rank] = total.astype(BF16)
+        return total
 
     def pass_sum():
-        arrived(row_recv.at[0, pl.ds(1, NY - 1)], ys_send.at[0], ys_recv.at[0])
-        cluster_sum(0, 0)
-        for dc in range(1, NC):
-            there = cc_all.at[0, :, pl.ds((NC - dc) * rank, rank)]
-            send(cc_all.at[0, :, pl.ds(0, rank)], there, cx_send, cx_recv, c_peer(dc, 0))
+        arrived(cc_all.at[0, :, pl.ds(rank, (NC - 1) * rank)], cx_send, cx_recv)
+        row_recv[0, 0] = dot_nt(cc_all[0], mmat[...]).astype(BF16)
+        for dy in (2, 1, 3):
+            send(row_recv.at[0, 0], row_recv.at[0, NY - dy], ys_send.at[0], ys_recv.at[0], y_peer(dy))
 
     def cluster_total(r):
         if r == 0:
-            arrived(cc_all.at[0, :, pl.ds(rank, (NC - 1) * rank)], cx_send, cx_recv)
+            arrived(row_recv.at[0, pl.ds(1, NY - 1)], ys_send.at[0], ys_recv.at[0])
+            total = column_sum(0, 0)
         else:
-            arrived(row_recv.at[r, pl.ds(1, NC * NY - 1)], ys_send.at[r], ys_recv.at[r])
+            arrived(row_recv.at[1, pl.ds(1, NC * NY - 1)], ys_send.at[1], ys_recv.at[1])
             for k in range(NC):
-                cluster_sum(r, k)
-        ct_all[r, mine] = dot_nt(cc_all[r], mmat[...]).astype(BF16)
+                cc_all[1, :, k * rank : (k + 1) * rank] = column_sum(1, k).astype(BF16)
+            total = dot_nt(cc_all[1], mmat[...])
+        far[r, mine, rank:] = total.astype(BF16)
+        there = far.at[r, mine, pl.ds(rank, rank)]
         for dz in (4, 3, 5, 2, 6, 1, 7):
-            send(ct_all.at[r, mine], ct_all.at[r, mine], ct_send.at[r], ct_recv.at[r], z_peer(dz))
+            send(there, there, ct_send.at[r], ct_recv.at[r], z_peer(dz))
 
     def early_sums(r):
         for h in range(2):
@@ -271,15 +280,13 @@
     def leaf_total(r):
         for h in range(2):
             arrived(part_recv.at[r, h, pl.ds(1, NY - 1)], pt_send.at[r], pt_recv.at[r, h])
-        totals = []
         for h in range(2):
-            total = acc[h * half : (h + 1) * half, 0:rank]
+            at = slice(h * half, (h + 1) * half)
+            total = acc[at, 0:rank]
             for k in range(1, NY):
                 total = total + part_recv[r, h, k].astype(F32)
-            totals.append(total)
-        total = jnp.concatenate(totals, axis=0)
-        arrived(ct_all.at[r, pl.ds(0, cols - piece)], ct_send.at[r], ct_recv.at[r])
-        return (total + dot_nt(ct_all[r], trans[...])).astype(BF16)
+            far[r, at, 0:rank] = total.astype(BF16)
+        arrived(far.at[r, pl.ds(0, cols - piece), pl.ds(rank, rank)], ct_send.at[r], ct_recv.at[r])
 
     def all_left(r):
         left(uterm_send.at[r, pl.ds(0, cols - piece)], rs_send.at[r], rs_recv.at[r])
@@ -289,7 +296,7 @@
             left(cc_all.at[r, :, pl.ds(rank, (NC - 1) * rank)], cx_send, cx_recv)
         else:
             left(row_recv.at[r, pl.ds(1, NC * NY - 1)], ys_send.at[r], ys_recv.at[r])
-        left(ct_all.at[r, pl.ds(0, cols - piece)], ct_send.at[r], ct_recv.at[r])
+        left(far.at[r, pl.ds(0, cols - piece), pl.ds(rank, rank)], ct_send.at[r], ct_recv.at[r])
         left(part_send.at[r, pl.ds(1, NY - 1)], pt_send.at[r], pt_recv.at[r, 0])
 
     def tiles(step, begin=0, end=TILES):
@@ -299,9 +306,12 @@
 
         lax.fori_loop(begin, end, run, 0)
 
+    loads["bases"].wait()
+    loads["trans"].wait()
+    rnb[:, rank : 2 * rank] = dot_nn(rnb[:, 0:rank], trans[...]).astype(BF16)
+    bases = rnb.at[:, pl.ds(0, 2 * rank)]
     loads["guess"].wait()
-    loads["bases"].wait()
-    start_exchange(0, dot_tn(bases[...], guess[...]).T.astype(BF16))
+    start_exchange(0, dot_tn(guess[...], bases[...]))
 
     loads["lists"].wait()
     loads["owner"].wait()
@@ -316,10 +326,9 @@
 
     loads["rhs"].wait()
     loads["diag"].wait()
-    rnb[:, cols : cols + rank] = bases[...]
 
     def near(at):
-        rnb[at, 0:cols] = (rhs[at].astype(F32) - dot_nn(diag[at], guess[...])).astype(BF16)
+        rnb[at, 2 * rank :] = (rhs[at].astype(F32) - dot_nn(diag[at], guess[...])).astype(BF16)
 
     tiles(near)
 
@@ -329,10 +338,11 @@
         emat[k] = dot_nn(mid[cluster], gcoup[k])
 
     def compose(k, carry):
-        other = lax.rem(cluster + k, NC)
+        there, also = flipped(k)
+        other = there * 2 + also
         pick = jnp.zeros((rank, rank), F32)
         for i in range(2):
-            pick = pick + jnp.where(glist_ref[0, i] == other // 2, 1.0, 0.0) * emat[i]
+            pick = pick + jnp.where(glist_ref[0, i] == there, 1.0, 0.0) * emat[i]
         value = dot_nt(pick.astype(BF16), mid[other])
         for i in range(3):
             value = value + jnp.where(clist_ref[0, i] == other, 1.0, 0.0) * ccoup[i].astype(F32)
@@ -344,17 +354,6 @@
     row_sum(0)
     relay(0, 0)
     relay(0, 1)
-
-    loads["prec"].wait()
-
-    def smooth(at):
-        both = dot_nn(prec[at], rnb[...])
-        base = guess[at].astype(F32) + damping * both[:, 0:cols]
-        first[at] = base
-        firsth[at] = base.astype(BF16)
-        pb[at] = both[:, cols : cols + rank].astype(BF16)
-
-    tiles(smooth, 0, 1)
     pass_sum()
 
     loads["coup"].wait()
@@ -374,26 +373,35 @@
 
     lax.fori_loop(0, NZ, place, 0)
     early_sums(0)
-    tiles(smooth, 1, 2)
     late_sums(0, 0)
     late_sums(0, 1)
     cluster_total(0)
-    tiles(smooth, 2, 3)
-    gmat[...] = dot_tn(bases[...], pb[...]).astype(BF16)
-    w_t[...] = dot_tn(bases[...], firsth[...]).T
-    far = leaf_total(0)
-
-    start_exchange(1, (w_t[...] - damping * dot_nt(far, gmat[...])).astype(BF16))
+
+    loads["prec"].wait()
+
+    def smooth(at):
+        both = dot_nn(prec[at], rnb[...])
+        base = guess[at].astype(F32) + damping * both[:, 2 * rank :]
+        first[at] = base
+        firsth[at] = base.astype(BF16)
+        pbx[at] = both[:, 0 : 2 * rank].astype(BF16)
+
+    tiles(smooth)
+    gmat[...] = dot_tn(bases[...], pbx[...]).astype(BF16)
+    w_t[...] = dot_tn(firsth[...], bases[...])
+    leaf_total(0)
+
+    start_exchange(1, w_t[...] - damping * dot_nt(far[0], gmat[...]))
 
     def correct(at):
-        value = first[at] - damping * dot_nt(pb[at], far)
+        value = first[at] - damping * dot_nt(pbx[at], far[0])
         first[at] = value
         firsth[at] = value.astype(BF16)
 
     correct(slice(0, n))
 
     def near_again(at):
-        rnb[at, 0:cols] = (rhs[at].astype(F32) - dot_nn(diag[at], firsth[...])).astype(BF16)
+        rnb[at, 2 * rank :] = (rhs[at].astype(F32) - dot_nn(diag[at], firsth[...])).astype(BF16)
 
     tiles(near_again)
     row_sum(1)
@@ -401,7 +409,7 @@
     relay(1, 1)
 
     def smooth_again(at):
-        first[at] = first[at] + damping * dot_nn(prec[at], rnb[:, 0:cols])
+        first[at] = first[at] + damping * dot_nn(prec[at], rnb[:, 2 * rank :])
 
     tiles(smooth_again)
     early_sums(1)
@@ -411,10 +419,10 @@
     all_left(0)
     left(meta_all.at[pl.ds(1, NY - 1)], wt_send.at[0], wt_recv.at[0])
     left(coup_all.at[pl.ds(1, NY - 1)], wt_send.at[1], wt_recv.at[1])
-    far = leaf_total(1)
+    leaf_total(1)
 
     def finish(at):
-        out_ref[at] = (first[at] - damping * dot_nt(pb[at], far)).astype(BF16)
+        out_ref[at] = (first[at] - damping * dot_nt(pbx[at], far[1])).astype(BF16)
 
     finish(slice(0, n))
     all_left(1)
@@ -455,7 +463,6 @@
             pltpu.VMEM((n, cols), BF16),
             pltpu.VMEM((n, n), BF16),
             pltpu.VMEM((n, n), BF16),
-            pltpu.VMEM((n, rank), BF16),
             pltpu.VMEM((rank, rank), BF16),
             pltpu.VMEM((NC, rank, rank), BF16),
             pltpu.VMEM((3, rank, rank), BF16),
@@ -465,19 +472,19 @@
             pltpu.VMEM((NY * rank, NZ * rank), BF16),
             pltpu.VMEM((rank, NC * rank), BF16),
             pltpu.VMEM((2, rank, rank), F32),
-            pltpu.VMEM((n, cols + rank), BF16),
+            pltpu.VMEM((n, cols + 2 * rank), BF16),
             pltpu.VMEM((n, cols), F32),
             pltpu.VMEM((n, cols), BF16),
-            pltpu.VMEM((n, rank), BF16),
-            pltpu.VMEM((rank, rank), BF16),
-            pltpu.VMEM((cols, rank), F32),
+            pltpu.VMEM((n, 2 * rank), BF16),
+            pltpu.VMEM((2 * rank, 2 * rank), BF16),
+            pltpu.VMEM((cols, 2 * rank), F32),
             pltpu.VMEM((cols, NY * rank), F32),
             pltpu.VMEM((2, cols, NZ * rank), BF16),
             pltpu.VMEM((2, cols, rank), BF16),
             pltpu.VMEM((2, NZ, piece, rank), BF16),
             pltpu.VMEM((2, NC * NY, piece, rank), BF16),
             pltpu.VMEM((2, piece, NC * rank), BF16),
-            pltpu.VMEM((2, cols, rank), BF16),
+            pltpu.VMEM((2, cols, 2 * rank), BF16),
             pltpu.VMEM((2, NY, cols, rank), BF16),
             pltpu.VMEM((2, 2, NY, cols // 2, rank), BF16),
             dma((14,)),

time: 45.5 us -> 44.2 us (0.971)
  Pallas kernels: 43.9 us -> 42.9 us
    pallas_call x1, Pallas kernels: 43.9 us -> 42.9 us  [body(): pl.pallas_call(kernel, out_shape=pltpu.VMEM((n, cols), BF16), in_specs=[h...]
where the time goes in v3:
time: 44.2 us; the launch traced here: 43.8 us
  Pallas kernels  42.9 us (97%)
  local copies, waits for them, and re-layouts  0.88 us (2%)
    pallas_call x1, Pallas kernels, body(): pl.pallas_call(kernel, out_shape=pltpu.VMEM((n, cols), BF16), in_specs=[h...  42.9 us

profile of v3, /device:TPU:32, one launch (start us, length us, event | category | flops | bytes accessed | tf_op | source)
XLA Modules:
  0.0 43.8 jit_solution(13314632650063587092)
XLA Ops:
  0.0 42.9 %shard_map.136 = bf16[1536,256]{1,0:T(8,128)(2,1)S(1)} custom-call(s32[1,4]{1,0:T(1,128)} %lists_hbm.1, s32[1,32]{1,0:T(1,128)} %owner_hbm.1, s32[1,3]{1,0:T(1,128)} %clist_hbm.1, s32[1,2]{1,0:T(1,128)} %glist_hbm.1, bf16[1536,256]{1,0:T(8,128)(2,1)} %rhs_hbm.1, bf16[1536,256]{1,0:T(8,128)(2,1)} %guess_hbm.1, bf16[1,1536,1536]{2,1,0:T(8,128)(2,1)} %diag_hbm.1, ...), custom_call_target="tpu_custom_call" | custom-call | tf_op jit(solution)/shard_map/pallas_call | solution.py:452
  42.9 0.9 %copy.16 = bf16[1536,256]{1,0:T(8,128)(2,1)} copy(bf16[1536,256]{1,0:T(8,128)(2,1)S(1)} %shard_map.136) | data formatting | bytes 1572864

commit v4 on v3

--- a/solution.py
+++ b/solution.py
@@ -12,6 +12,8 @@
 ABROAD = [(k, dy) for k in range(NC) for dy in range(NY) if k or dy]
 ABROAD.sort(key=lambda p: -((0, 2, 0, 2, 1, 1, 1, 1)[p[0]] + (0, 1, 2, 1)[p[1]]))
 PLACE = {0: 0, 1: 1, 7: 2, 2: 3, 6: 4, 3: 5, 5: 6, 4: 7}
+PLACES = [(1, 3), (3, 4), (4, 5), (5, 8)]
+STEP = {k: next(i for i, (begin, end) in enumerate(PLACES) if begin <= at < end) for k, at in PLACE.items() if k}
 F32, BF16 = jnp.float32, jnp.bfloat16
 
 
@@ -73,6 +75,9 @@
     row_recv,
     cc_all,
     far,
+    loop_send,
+    loop_recv,
+    loop_row,
     part_send,
     part_recv,
     load_sem,
@@ -88,6 +93,8 @@
     cx_recv,
     ct_send,
     ct_recv,
+    lp_send,
+    lp_recv,
     pt_send,
     pt_recv,
 ):
@@ -98,6 +105,7 @@
     rank = trans.shape[1]
     piece = cols // NZ
     half = cols // 2
+    strip = rank // NZ
     tile = n // TILES
 
     def z_peer(dz):
@@ -117,8 +125,10 @@
     barrier = pltpu.get_barrier_semaphore()
     for dz in (4, 3, 5, 2, 6, 1, 7):
         pl.semaphore_signal(barrier, inc=1, device_id=z_peer(dz), device_id_type=MESH)
-    for dc, dy in ABROAD:
-        pl.semaphore_signal(barrier, inc=1, device_id=c_peer(dc, dy), device_id_type=MESH)
+    for dy in (2, 1, 3):
+        pl.semaphore_signal(barrier, inc=1, device_id=y_peer(dy), device_id_type=MESH)
+    for k in (1, 3, 4, 5, 6, 7, 2):
+        pl.semaphore_signal(barrier, inc=1, device_id=c_peer(k, 0), device_id_type=MESH)
 
     loads = {}
     for i, (name, src, dst) in enumerate(
@@ -126,17 +136,17 @@
             ("bases", bases_hbm.at[0], rnb.at[:, pl.ds(0, rank)]),
             ("trans", trans_hbm.at[0], trans),
             ("guess", guess_hbm, guess),
+            ("coup", coup_hbm.at[0], coup_all.at[0]),
             ("lists", lists_hbm, lists_ref),
             ("owner", owner_hbm, owner_ref),
             ("clist", clist_hbm, clist_ref),
             ("glist", glist_hbm, glist_ref),
-            ("rhs", rhs_hbm, rhs),
-            ("diag", diag_hbm.at[0], diag),
             ("mid", mid_hbm, mid),
             ("ccoup", ccoup_hbm.at[0], ccoup),
             ("gcoup", gcoup_hbm.at[0], gcoup),
-            ("coup", coup_hbm.at[0], coup_all.at[0]),
             ("prec", prec_hbm.at[0], prec),
+            ("diag", diag_hbm.at[0], diag),
+            ("rhs", rhs_hbm, rhs),
         )
     ):
         loads[name] = pltpu.make_async_copy(src, dst, load_sem.at[i])
@@ -179,16 +189,13 @@
         return coef.at[r, pl.ds(h * half, half), pl.ds(PLACE[k] * rank, rank)]
 
     def pass_on(r, h, source, k, dz):
-        send(block(r, h, source), block(r, h, k), ag_send.at[r], ag_recv.at[r, h, k], z_peer(dz))
-
-    def here(r, h, k):
-        arrived(block(r, h, k), ag_send.at[r], ag_recv.at[r, h, k])
-
-    def start_exchange(r, both):
-        coef[r, :, 0:rank] = both[:, 0:rank].astype(BF16)
-        uterm_send[r] = both[:, rank:].astype(BF16)
-        if r == 0:
-            pl.semaphore_wait(barrier, NZ - 1 + len(ABROAD))
+        send(block(r, h, source), block(r, h, k), ag_send.at[r], ag_recv.at[r, h, STEP[k]], z_peer(dz))
+
+    def here(r, h, begin, end):
+        blocks = coef.at[r, pl.ds(h * half, half), pl.ds(begin * rank, (end - begin) * rank)]
+        arrived(blocks, ag_send.at[r], ag_recv.at[r, h, PLACES.index((begin, end))])
+
+    def send_terms(r):
         for dz in (4, 3, 5, 2, 6, 1, 7):
             there = lax.rem(z + dz, NZ)
             send(
@@ -198,16 +205,34 @@
                 rs_recv.at[r],
                 z_peer(dz),
             )
+
+    def send_coefs(r):
         for dz in (2, 6, 1, 7):
             for h in range(2):
                 pass_on(r, h, 0, NZ - dz, dz)
 
+    def send_loop():
+        loop_send[...] = gmat[rank:, rank:]
+        for dz in (4, 3, 5, 2, 6, 1, 7):
+            there = pl.ds(pl.multiple_of(lax.rem(z + dz, NZ) * strip, strip), strip)
+            send(loop_send.at[there], loop_recv.at[NZ - dz], lp_send.at[0], lp_recv.at[0], z_peer(dz))
+
+    def pass_loop():
+        arrived(loop_recv.at[pl.ds(1, NZ - 1)], lp_send.at[0], lp_recv.at[0])
+        own = pl.ds(pl.multiple_of(z * strip, strip), strip)
+        total = loop_send[own].astype(F32)
+        for k in range(1, NZ):
+            total = total + loop_recv[k].astype(F32)
+        loop_row[own] = total.astype(BF16)
+        for dz in (4, 3, 5, 2, 6, 1, 7):
+            send(loop_row.at[own], loop_row.at[own], lp_send.at[1], lp_recv.at[1], z_peer(dz))
+
     def relay(r, h):
-        here(r, h, 6)
+        here(r, h, 4, 5)
         if h == 0:
             pass_on(r, h, 6, 4, 2)
         pass_on(r, h, 6, 5, 1)
-        here(r, h, 2)
+        here(r, h, 3, 4)
         if h == 1:
             pass_on(r, h, 2, 4, 6)
         pass_on(r, h, 2, 3, 7)
@@ -217,6 +242,9 @@
         total = uterm_send[r, mine].astype(F32)
         for k in range(1, NZ):
             total = total + uterm_recv[r, k].astype(F32)
+        if r == 1:
+            arrived(loop_row.at[pl.ds(0, rank - strip)], lp_send.at[1], lp_recv.at[1])
+            total = total - damping * dot_nt(far[0, mine, rank:], loop_row[...])
         if r == 0:
             cc_all[0, :, 0:rank] = total.astype(BF16)
             for k in (1, 3, 4, 5, 6, 7, 2):
@@ -256,15 +284,17 @@
 
     def early_sums(r):
         for h in range(2):
-            here(r, h, 1)
-            here(r, h, 7)
+            here(r, h, 1, 3)
         acc[...] = dot_nt(coef[r, :, 0 : 5 * rank], weights[:, 0 : 5 * rank])
 
     def late_sums(r, h):
-        for k in (3, 5, 4):
-            here(r, h, k)
+        here(r, h, 5, 8)
         rows = slice(h * half, (h + 1) * half)
-        value = acc[rows] + dot_nt(coef[r, rows, 5 * rank :], weights[:, 5 * rank :])
+        if r == 0:
+            here(r, h, 1, 3)
+            value = dot_nt(coef[r, rows], weights[...])
+        else:
+            value = acc[rows] + dot_nt(coef[r, rows, 5 * rank :], weights[:, 5 * rank :])
         acc[rows, 0:rank] = value[:, 0:rank]
         for j in (2, 1, 3):
             part_send[r, j, rows] = value[:, j * rank : (j + 1) * rank].astype(BF16)
@@ -277,7 +307,7 @@
                 y_peer(j),
             )
 
-    def leaf_total(r):
+    def leaf_sum(r):
         for h in range(2):
             arrived(part_recv.at[r, h, pl.ds(1, NY - 1)], pt_send.at[r], pt_recv.at[r, h])
         for h in range(2):
@@ -286,6 +316,8 @@
             for k in range(1, NY):
                 total = total + part_recv[r, h, k].astype(F32)
             far[r, at, 0:rank] = total.astype(BF16)
+
+    def gather_total(r):
         arrived(far.at[r, pl.ds(0, cols - piece), pl.ds(rank, rank)], ct_send.at[r], ct_recv.at[r])
 
     def all_left(r):
@@ -311,8 +343,14 @@
     rnb[:, rank : 2 * rank] = dot_nn(rnb[:, 0:rank], trans[...]).astype(BF16)
     bases = rnb.at[:, pl.ds(0, 2 * rank)]
     loads["guess"].wait()
-    start_exchange(0, dot_tn(guess[...], bases[...]))
-
+    both = dot_tn(guess[...], bases[...]).astype(BF16)
+    uterm_send[0] = both[:, rank:]
+    coef[0, :, 0:rank] = both[:, 0:rank]
+    pl.semaphore_wait(barrier, NZ + NY + NC - 3)
+    send_terms(0)
+    send_coefs(0)
+
+    loads["coup"].wait()
     loads["lists"].wait()
     loads["owner"].wait()
     rows = lax.broadcasted_iota(jnp.int32, (8, rank), 0)
@@ -321,16 +359,8 @@
         meta = jnp.where(rows == k, owner_ref[0, lists_ref[0, k]], meta)
     meta_all[0] = meta
     for dy in (2, 1, 3):
-        send(coup_hbm.at[0], coup_all.at[NY - dy], wt_send.at[1], wt_recv.at[1], y_peer(dy))
+        send(coup_all.at[0], coup_all.at[NY - dy], wt_send.at[1], wt_recv.at[1], y_peer(dy))
         send(meta_all.at[0], meta_all.at[NY - dy], wt_send.at[0], wt_recv.at[0], y_peer(dy))
-
-    loads["rhs"].wait()
-    loads["diag"].wait()
-
-    def near(at):
-        rnb[at, 2 * rank :] = (rhs[at].astype(F32) - dot_nn(diag[at], guess[...])).astype(BF16)
-
-    tiles(near)
 
     for name in ("mid", "gcoup", "ccoup", "clist", "glist"):
         loads[name].wait()
@@ -351,12 +381,27 @@
 
     lax.fori_loop(0, NC, compose, 0)
 
+    loads["prec"].wait()
+
+    def smooth_bases(at):
+        pbx[at] = dot_nn(prec[at], bases[...]).astype(BF16)
+
+    tiles(smooth_bases)
+    gmat[...] = dot_tn(bases[...], pbx[...]).astype(BF16)
+    send_loop()
+
     row_sum(0)
     relay(0, 0)
     relay(0, 1)
-    pass_sum()
-
-    loads["coup"].wait()
+
+    loads["rhs"].wait()
+    loads["diag"].wait()
+
+    def near(at):
+        rnb[at, 2 * rank :] = (rhs[at].astype(F32) - dot_nn(diag[at], guess[...])).astype(BF16)
+
+    tiles(near, 0, 2)
+
     arrived(meta_all.at[pl.ds(1, NY - 1)], wt_send.at[0], wt_recv.at[0])
     arrived(coup_all.at[pl.ds(1, NY - 1)], wt_send.at[1], wt_recv.at[1])
 
@@ -364,34 +409,34 @@
         away = ((p + 1) // 2) * (2 * lax.rem(p, 2) - 1)
         slot = y * NZ + lax.rem(z + away + NZ, NZ)
         for j in range(NY):
-            hit = jnp.where(meta_all[j] == slot, 1.0, 0.0)
-            value = jnp.zeros((rank, rank), F32)
-            for i in range(4):
-                value = value + hit[i : i + 1] * coup_all[j, i].astype(F32)
-            weights[j * rank : (j + 1) * rank, pl.ds(pl.multiple_of(p * rank, rank), rank)] = value.astype(BF16)
+            hit = jnp.where(meta_all[j] == slot, 1.0, 0.0).astype(BF16)
+            value = hit[0:1] * coup_all[j, 0]
+            for i in range(1, 4):
+                value = value + hit[i : i + 1] * coup_all[j, i]
+            weights[j * rank : (j + 1) * rank, pl.ds(pl.multiple_of(p * rank, rank), rank)] = value
         return carry
 
     lax.fori_loop(0, NZ, place, 0)
-    early_sums(0)
+    pass_sum()
     late_sums(0, 0)
     late_sums(0, 1)
+    tiles(near, 2, 3)
     cluster_total(0)
-
-    loads["prec"].wait()
+    pass_loop()
 
     def smooth(at):
-        both = dot_nn(prec[at], rnb[...])
-        base = guess[at].astype(F32) + damping * both[:, 2 * rank :]
+        base = guess[at].astype(F32) + damping * dot_nn(prec[at], rnb[:, 2 * rank :])
         first[at] = base
         firsth[at] = base.astype(BF16)
-        pbx[at] = both[:, 0 : 2 * rank].astype(BF16)
 
     tiles(smooth)
-    gmat[...] = dot_tn(bases[...], pbx[...]).astype(BF16)
     w_t[...] = dot_tn(firsth[...], bases[...])
-    leaf_total(0)
-
-    start_exchange(1, w_t[...] - damping * dot_nt(far[0], gmat[...]))
+    leaf_sum(0)
+    uterm_send[1] = (w_t[:, rank:] - damping * dot_nt(far[0, :, 0:rank], gmat[rank:, 0:rank])).astype(BF16)
+    send_terms(1)
+    gather_total(0)
+    coef[1, :, 0:rank] = (w_t[:, 0:rank] - damping * dot_nt(far[0], gmat[0:rank])).astype(BF16)
+    send_coefs(1)
 
     def correct(at):
         value = first[at] - damping * dot_nt(pbx[at], far[0])
@@ -417,9 +462,12 @@
     late_sums(1, 1)
     cluster_total(1)
     all_left(0)
+    left(loop_send.at[pl.ds(0, rank - strip)], lp_send.at[0], lp_recv.at[0])
+    left(loop_row.at[pl.ds(0, rank - strip)], lp_send.at[1], lp_recv.at[1])
     left(meta_all.at[pl.ds(1, NY - 1)], wt_send.at[0], wt_recv.at[0])
     left(coup_all.at[pl.ds(1, NY - 1)], wt_send.at[1], wt_recv.at[1])
-    leaf_total(1)
+    leaf_sum(1)
+    gather_total(1)
 
     def finish(at):
         out_ref[at] = (first[at] - damping * dot_nt(pbx[at], far[1])).astype(BF16)
@@ -485,19 +533,24 @@
             pltpu.VMEM((2, NC * NY, piece, rank), BF16),
             pltpu.VMEM((2, piece, NC * rank), BF16),
             pltpu.VMEM((2, cols, 2 * rank), BF16),
+            pltpu.VMEM((rank, rank), BF16),
+            pltpu.VMEM((NZ, rank // NZ, rank), BF16),
+            pltpu.VMEM((rank, rank), BF16),
             pltpu.VMEM((2, NY, cols, rank), BF16),
             pltpu.VMEM((2, 2, NY, cols // 2, rank), BF16),
             dma((14,)),
             dma((2,)),
             dma((2,)),
             dma((2,)),
-            dma((2, 2, NZ)),
+            dma((2, 2, len(PLACES))),
             dma((2,)),
             dma((2,)),
             dma((2,)),
             dma((2,)),
             dma,
             dma,
+            dma((2,)),
+            dma((2,)),
             dma((2,)),
             dma((2,)),
             dma((2,)),

time: 44.2 us -> 42.8 us (0.968)
  Pallas kernels: 42.9 us -> 41.5 us
    pallas_call x1, Pallas kernels: 42.9 us -> 41.5 us  [body(): pl.pallas_call(kernel, out_shape=pltpu.VMEM((n, cols), BF16), in_specs=[h...]
where the time goes in v4:
time: 42.8 us; the launch traced here: 42.4 us
  Pallas kernels  41.5 us (97%)
  local copies, waits for them, and re-layouts  0.88 us (2%)
    pallas_call x1, Pallas kernels, body(): pl.pallas_call(kernel, out_shape=pltpu.VMEM((n, cols), BF16), in_specs=[h...  41.5 us
    unnamed x1, local copies, waits for them, and re-layouts  0.88 us

profile of v4, /device:TPU:32, one launch (start us, length us, event | category | flops | bytes accessed | tf_op | source)
XLA Modules:
  0.0 42.4 jit_solution(8456535863677248505)
XLA Ops:
  0.0 41.5 %shard_map.136 = bf16[1536,256]{1,0:T(8,128)(2,1)S(1)} custom-call(s32[1,4]{1,0:T(1,128)} %lists_hbm.1, s32[1,32]{1,0:T(1,128)} %owner_hbm.1, s32[1,3]{1,0:T(1,128)} %clist_hbm.1, s32[1,2]{1,0:T(1,128)} %glist_hbm.1, bf16[1536,256]{1,0:T(8,128)(2,1)} %rhs_hbm.1, bf16[1536,256]{1,0:T(8,128)(2,1)} %guess_hbm.1, bf16[1,1536,1536]{2,1,0:T(8,128)(2,1)} %diag_hbm.1, ...), custom_call_target="tpu_custom_call" | custom-call | tf_op jit(solution)/shard_map/pallas_call | solution.py:500
  41.5 0.9 %copy.16 = bf16[1536,256]{1,0:T(8,128)(2,1)} copy(bf16[1536,256]{1,0:T(8,128)(2,1)S(1)} %shard_map.136) | data formatting | bytes 1572864

commit v5 on v4

--- a/solution.py
+++ b/solution.py
@@ -388,11 +388,11 @@
 
     tiles(smooth_bases)
     gmat[...] = dot_tn(bases[...], pbx[...]).astype(BF16)
-    send_loop()
 
     row_sum(0)
     relay(0, 0)
     relay(0, 1)
+    send_loop()
 
     loads["rhs"].wait()
     loads["diag"].wait()
@@ -418,9 +418,9 @@
 
     lax.fori_loop(0, NZ, place, 0)
     pass_sum()
+    tiles(near, 2, 3)
     late_sums(0, 0)
     late_sums(0, 1)
-    tiles(near, 2, 3)
     cluster_total(0)
     pass_loop()
 

time: 42.8 us -> 43.1 us (level)
  Pallas kernels: 41.5 us -> 42.1 us
    pallas_call x1, Pallas kernels: 41.5 us -> 42.1 us  [body(): pl.pallas_call(kernel, out_shape=pltpu.VMEM((n, cols), BF16), in_specs=[h...]
where the time goes in v5:
time: 43.1 us; the launch traced here: 43 us
  Pallas kernels  42.1 us (98%)
  local copies, waits for them, and re-layouts  0.88 us (2%)
    pallas_call x1, Pallas kernels, body(): pl.pallas_call(kernel, out_shape=pltpu.VMEM((n, cols), BF16), in_specs=[h...  42.1 us
    unnamed x1, local copies, waits for them, and re-layouts  0.88 us

profile of v5, /device:TPU:32, one launch (start us, length us, event | category | flops | bytes accessed | tf_op | source)
XLA Modules:
  0.0 43.0 jit_solution(1670926625362593741)
XLA Ops:
  0.0 42.1 %shard_map.136 = bf16[1536,256]{1,0:T(8,128)(2,1)S(1)} custom-call(s32[1,4]{1,0:T(1,128)} %lists_hbm.1, s32[1,32]{1,0:T(1,128)} %owner_hbm.1, s32[1,3]{1,0:T(1,128)} %clist_hbm.1, s32[1,2]{1,0:T(1,128)} %glist_hbm.1, bf16[1536,256]{1,0:T(8,128)(2,1)} %rhs_hbm.1, bf16[1536,256]{1,0:T(8,128)(2,1)} %guess_hbm.1, bf16[1,1536,1536]{2,1,0:T(8,128)(2,1)} %diag_hbm.1, ...), custom_call_target="tpu_custom_call" | custom-call | tf_op jit(solution)/shard_map/pallas_call | solution.py:500
  42.1 0.9 %copy.16 = bf16[1536,256]{1,0:T(8,128)(2,1)} copy(bf16[1536,256]{1,0:T(8,128)(2,1)S(1)} %shard_map.136) | data formatting | bytes 1572864
